TPU v7x, 32 devices: a 4x2x2 block of a 4x4x8 slice. The times are simulated.
32 devices in a mesh: dp: 4 (over y, z), tp: 8 (over x, core).
Axes of the slice: x: 4, y: 2, z: 2, core: 2. Of those that a mesh axis runs over, the one named last changes fastest.
The devices are a block of a 4x4x8 slice.
Arguments:
- hidden: bfloat16 [32, 2048, 1024], P('dp', 'tp'), parts along dimension 0
- attn_gain: float32 [1024], replicated
- attn_bias: float32 [1024], replicated
- mlp_gain: float32 [1024], replicated
- mlp_bias: float32 [1024], replicated
- w_qkv: bfloat16 [1024, 16, 192], P(None, 'tp')
- w_out: bfloat16 [1024, 1024], P('tp')
- w_up: bfloat16 [1024, 4096], P(None, 'tp')
- w_down: bfloat16 [4096, 1024], P('tp')
- positions: int32 [2048], replicated
Outputs:
- output: bfloat16 [32, 2048, 1024], P('dp', 'tp'), parts along dimension 0
There are 4 independent parts. A program takes and returns all parts, laid end to end along the dimension named above; an argument that names none is the same for every part.
All inputs are finite; a program needn't handle non-finite values.
Results may differ from a plain program's by a relative error of at most 0.00413463.
Values are sent between devices in bfloat16 or wider.
A program may use at most 768 MiB of HBM per device.

v0:
```python
import jax
import jax.numpy as jnp
from jax import lax
from jax.sharding import PartitionSpec as P


def layer_norm(tok_rows, norm_gain, norm_bias):
    rows32 = tok_rows.astype(jnp.float32)
    row_mean = jnp.mean(rows32, axis=-1, keepdims=True)
    centered = rows32 - row_mean
    row_var = jnp.mean(centered * centered, axis=-1, keepdims=True)
    return (centered * lax.rsqrt(row_var + 1e-5) * norm_gain + norm_bias).astype(jnp.bfloat16)


def rotary_tables(positions, head_dim):
    inv_freq = 10000.0 ** (-2.0 * jnp.arange(head_dim // 2, dtype=jnp.float32) / head_dim)
    angles = positions.astype(jnp.float32)[:, None] * inv_freq[None, :]
    angles = jnp.concatenate([angles, angles], axis=-1)
    return jnp.cos(angles), jnp.sin(angles)


def apply_rotary(head_vals, cos_tab, sin_tab):
    half_dim = head_vals.shape[-1] // 2
    vals32 = head_vals.astype(jnp.float32)
    rotated = jnp.concatenate([-vals32[..., half_dim:], vals32[..., :half_dim]], axis=-1)
    return (vals32 * cos_tab + rotated * sin_tab).astype(jnp.bfloat16)


def attention_branch(normed, w_qkv_part, w_out_part, positions):
    batch_size, seq_len, model_width = normed.shape
    num_groups = w_qkv_part.shape[1]
    slot_cols = w_qkv_part.shape[2]
    group_cols = w_out_part.shape[0] // num_groups
    head_dim = (slot_cols - group_cols) // 2
    group_size = group_cols // head_dim
    qkv_rows = jnp.einsum('bsd,dkc->bskc', normed, w_qkv_part, preferred_element_type=jnp.float32).astype(jnp.bfloat16)
    qkv_rows = qkv_rows.reshape(batch_size, seq_len, num_groups, group_size + 2, head_dim)
    cos_tab, sin_tab = rotary_tables(positions, head_dim)
    query_rot = apply_rotary(qkv_rows[:, :, :, :group_size, :], cos_tab[None, :, None, None, :], sin_tab[None, :, None, None, :])
    key_rot = apply_rotary(qkv_rows[:, :, :, group_size, :], cos_tab[None, :, None, :], sin_tab[None, :, None, :])
    value_seq = qkv_rows[:, :, :, group_size + 1, :]
    block_len = min(seq_len, 256)
    num_blocks = seq_len // block_len
    key_idx = jnp.arange(seq_len)
    score_scale = head_dim ** -0.5

    def one_block(block_idx):
        row_start = block_idx * block_len
        query_blk = lax.dynamic_slice_in_dim(query_rot, row_start, block_len, axis=1)
        scores = jnp.einsum('bqkgh,bskh->bkgqs', query_blk, key_rot, preferred_element_type=jnp.float32) * score_scale
        query_idx = row_start + jnp.arange(block_len)
        allowed = key_idx[None, :] <= query_idx[:, None]
        scores = jnp.where(allowed, scores, -1e30)
        exp_scores = jnp.exp(scores - jnp.max(scores, axis=-1, keepdims=True))
        attn_probs = (exp_scores / jnp.sum(exp_scores, axis=-1, keepdims=True)).astype(jnp.bfloat16)
        context = jnp.einsum('bkgqs,bskh->bqkgh', attn_probs, value_seq, preferred_element_type=jnp.float32)
        return context.astype(jnp.bfloat16).reshape(batch_size, block_len, num_groups * group_cols)

    ctx_blocks = lax.map(one_block, jnp.arange(num_blocks))
    attn_part = jnp.einsum('nbqc,cd->bnqd', ctx_blocks, w_out_part, preferred_element_type=jnp.float32)
    return attn_part.reshape(batch_size, seq_len, model_width)


def solution(mesh):
    def local_layer(hidden_blk, attn_gain, attn_bias, mlp_gain, mlp_bias, w_qkv_part, w_out_part, w_up_part, w_down_part, positions):
        normed_attn = layer_norm(hidden_blk, attn_gain, attn_bias)
        normed_mlp = layer_norm(hidden_blk, mlp_gain, mlp_bias)
        attn_in = lax.all_gather(normed_attn, 'tp', axis=1, tiled=True)
        mlp_in = lax.all_gather(normed_mlp, 'tp', axis=1, tiled=True)
        attn_part = attention_branch(attn_in, w_qkv_part, w_out_part, positions)
        up_pre = jnp.einsum('bsd,df->bsf', mlp_in, w_up_part, preferred_element_type=jnp.float32)
        up_act = jax.nn.gelu(up_pre, approximate=False).astype(jnp.bfloat16)
        mlp_part = jnp.einsum('bsf,fd->bsd', up_act, w_down_part, preferred_element_type=jnp.float32)
        token_sum = lax.psum_scatter(attn_part + mlp_part, 'tp', scatter_dimension=1, tiled=True)
        return (hidden_blk.astype(jnp.float32) + token_sum).astype(jnp.bfloat16)

    return jax.shard_map(local_layer, mesh=mesh, in_specs=(P('dp', 'tp', None), P(), P(), P(), P(), P(None, 'tp', None), P('tp', None), P(None, 'tp'), P('tp', None), P()), out_specs=P('dp', 'tp', None), check_vma=False)
```

profile of v0, /device:TPU:81, one launch (start us, length us, event | category | flops | bytes accessed | tf_op | source)
XLA Modules:
  0.0 1192.9 jit_solution(7174401265868696612)
XLA Ops:
  6.6 2.9 convert_reduce_fusion
  9.5 3.0 fusion.66
  12.5 6.5 fusion.65
  19.1 0.7 all-gather.5.cloned.1.call-update
  20.1 0.7 convert_element_type.57
  20.9 2.6 fusion.86
  23.5 153.9 %all-gather.3.cloned.1.call-done = bf16[8,2048,1024]{2,1,0:T(8,128)(2,1)} async-done(((bf16[8,256,1024]{2,1,0:T(8,128)(2,1)}), bf16[8,2048,1024]{2,1,0:T(8,128)(2,1)}) %all-gather.3.cloned.1.call-update) | async-done | bytes 33554448 | tf_op jit(solution)/shard_map/all_gather | solution.py:68
  177.4 46.2 %fusion.74 = bf16[8,2048,2,192]{1,3,2,0:T(8,128)(2,1)} fusion(bf16[8,2048,1024]{2,1,0:T(8,128)(2,1)} %all-gather.3.cloned.1.call-done, bf16[1024,2,192]{0,2,1:T(8,128)(2,1)} %param.17), kind=kOutput, calls=%fused_computation.96 | convolution fusion | flops 12891193344 | bytes 46923776 | tf_op jit(solution)/shard_map/bsd,dkc->bskc/dot_general | solution.py:36
  223.5 10.5 slice_bitcast_fusion
  234.0 8.3 slice_negate_fusion
  242.3 4.0 slice_negate_fusion.1
  246.3 6.1 fusion.71
  252.4 5.9 fusion.69
  258.2 393.4 %while.11 = (s32[]{:T(128)}, bf16[8,8,256,128]{2,3,1,0:T(8,128)(2,1)}, s32[8]{0:T(128)S(1)}, bf16[8,2048,2,1,64]{1,4,2,0,3:T(8,128)(2,1)}, bf16[8,2048,2,64]{1,3...) while((s32[]{:T(128)}, ...), condition=%wide.region_5.6_spmd.clone, body=%wide.region_2.5_spmd.clone.sunk | while | flops 2248925440 | bytes 113330360 | solution.py:59
  258.2 0.6 dynamic_slice.18
  259.4 0.4 iota_compare_fusion.2
  259.7 15.5 %fusion.135 = (f32[8,2,256]{2,1,0:T(2,128)S(1)}, f32[8,2,256,2048]{3,2,1,0:T(8,128)}) fusion(pred[256,2048]{1,0:T(8,128)(4,1)S(1)} %iota_compare_fusion.2, bf16[8,2048,2,64]{1,3,2,0:T(8,128)(2,1)} %get-tuple-element.150, bf16[8,2048,2,1,64]{1,4,2,0,3:T(8,128)(2,1)} %get-tuple-element.149, s32[]{:T(128)S(6)} %select_n.28), kind=kOutput, calls=%fused_computation.5.clone.1 | convolution fusion | flops 1098903552 | bytes 38813700 | tf_op jit(solution)/shard_map/while/body/eval_jaxpr/bqkgh,bskh->bkgqs/dot_general | solution.py:50
  275.2 15.0 %fusion.136 = f32[8,2,256]{2,1,0:T(2,128)S(1)} fusion(f32[8,2,256,2048]{3,2,1,0:T(8,128)} %get-tuple-element.124, f32[8,2,256]{2,1,0:T(2,128)S(1)} %get-tuple-element.125, pred[256,2048]{1,0:T(8,128)(4,1)S(1)} %iota_compare_fusion.2), kind=kLoop, calls=%fused_computation.4.clone.1 | loop fusion | flops 33550336 | bytes 34111488 | tf_op jit(solution)/shard_map/while/body/eval_jaxpr/reduce_sum | solution.py:55
  290.2 16.3 %fusion.137 = bf16[8,2,256,64]{2,3,1,0:T(8,128)(2,1)S(1)} fusion(bf16[8,2048,2,64]{1,3,2,0:T(8,128)(2,1)} %get-tuple-element.151, f32[8,2,256]{2,1,0:T(2,128)S(1)} %fusion.136, f32[8,2,256]{2,1,0:T(2,128)S(1)} %get-tuple-element.125, f32[8,2,256,2048]{3,2,1,0:T(8,128)} %get-tuple-element.124, pred[256,2048]{1,0:T(8,128)(4,1)S(1)} %iota_compare_fusion.2), kind=kOutput, calls=%fused_computation.9.clone.1 | convolution fusion | flops 1115947008 | bytes 38830080 | tf_op jit(solution)/shard_map/while/body/eval_jaxpr/bkgqs,bskh->bqkgh/dot_general | solution.py:56
  306.6 0.8 constant_dynamic-update-slice_fusion.2
  307.4 0.6 dynamic_slice.18
  308.6 0.4 iota_compare_fusion.2
  308.9 15.5 %fusion.135 = (f32[8,2,256]{2,1,0:T(2,128)S(1)}, f32[8,2,256,2048]{3,2,1,0:T(8,128)}) fusion(pred[256,2048]{1,0:T(8,128)(4,1)S(1)} %iota_compare_fusion.2, bf16[8,2048,2,64]{1,3,2,0:T(8,128)(2,1)} %get-tuple-element.150, bf16[8,2048,2,1,64]{1,4,2,0,3:T(8,128)(2,1)} %get-tuple-element.149, s32[]{:T(128)S(6)} %select_n.28), kind=kOutput, calls=%fused_computation.5.clone.1 | convolution fusion | flops 1098903552 | bytes 38813700 | tf_op jit(solution)/shard_map/while/body/eval_jaxpr/bqkgh,bskh->bkgqs/dot_general | solution.py:50
  324.4 15.0 %fusion.136 = f32[8,2,256]{2,1,0:T(2,128)S(1)} fusion(f32[8,2,256,2048]{3,2,1,0:T(8,128)} %get-tuple-element.124, f32[8,2,256]{2,1,0:T(2,128)S(1)} %get-tuple-element.125, pred[256,2048]{1,0:T(8,128)(4,1)S(1)} %iota_compare_fusion.2), kind=kLoop, calls=%fused_computation.4.clone.1 | loop fusion | flops 33550336 | bytes 34111488 | tf_op jit(solution)/shard_map/while/body/eval_jaxpr/reduce_sum | solution.py:55
  339.4 16.3 %fusion.137 = bf16[8,2,256,64]{2,3,1,0:T(8,128)(2,1)S(1)} fusion(bf16[8,2048,2,64]{1,3,2,0:T(8,128)(2,1)} %get-tuple-element.151, f32[8,2,256]{2,1,0:T(2,128)S(1)} %fusion.136, f32[8,2,256]{2,1,0:T(2,128)S(1)} %get-tuple-element.125, f32[8,2,256,2048]{3,2,1,0:T(8,128)} %get-tuple-element.124, pred[256,2048]{1,0:T(8,128)(4,1)S(1)} %iota_compare_fusion.2), kind=kOutput, calls=%fused_computation.9.clone.1 | convolution fusion | flops 1115947008 | bytes 38830080 | tf_op jit(solution)/shard_map/while/body/eval_jaxpr/bkgqs,bskh->bqkgh/dot_general | solution.py:56
  355.7 0.8 constant_dynamic-update-slice_fusion.2
  356.6 0.6 dynamic_slice.18
  358.1 15.5 %fusion.135 = (f32[8,2,256]{2,1,0:T(2,128)S(1)}, f32[8,2,256,2048]{3,2,1,0:T(8,128)}) fusion(pred[256,2048]{1,0:T(8,128)(4,1)S(1)} %iota_compare_fusion.2, bf16[8,2048,2,64]{1,3,2,0:T(8,128)(2,1)} %get-tuple-element.150, bf16[8,2048,2,1,64]{1,4,2,0,3:T(8,128)(2,1)} %get-tuple-element.149, s32[]{:T(128)S(6)} %select_n.28), kind=kOutput, calls=%fused_computation.5.clone.1 | convolution fusion | flops 1098903552 | bytes 38813700 | tf_op jit(solution)/shard_map/while/body/eval_jaxpr/bqkgh,bskh->bkgqs/dot_general | solution.py:50
  373.6 15.0 %fusion.136 = f32[8,2,256]{2,1,0:T(2,128)S(1)} fusion(f32[8,2,256,2048]{3,2,1,0:T(8,128)} %get-tuple-element.124, f32[8,2,256]{2,1,0:T(2,128)S(1)} %get-tuple-element.125, pred[256,2048]{1,0:T(8,128)(4,1)S(1)} %iota_compare_fusion.2), kind=kLoop, calls=%fused_computation.4.clone.1 | loop fusion | flops 33550336 | bytes 34111488 | tf_op jit(solution)/shard_map/while/body/eval_jaxpr/reduce_sum | solution.py:55
  388.6 16.3 %fusion.137 = bf16[8,2,256,64]{2,3,1,0:T(8,128)(2,1)S(1)} fusion(bf16[8,2048,2,64]{1,3,2,0:T(8,128)(2,1)} %get-tuple-element.151, f32[8,2,256]{2,1,0:T(2,128)S(1)} %fusion.136, f32[8,2,256]{2,1,0:T(2,128)S(1)} %get-tuple-element.125, f32[8,2,256,2048]{3,2,1,0:T(8,128)} %get-tuple-element.124, pred[256,2048]{1,0:T(8,128)(4,1)S(1)} %iota_compare_fusion.2), kind=kOutput, calls=%fused_computation.9.clone.1 | convolution fusion | flops 1115947008 | bytes 38830080 | tf_op jit(solution)/shard_map/while/body/eval_jaxpr/bkgqs,bskh->bqkgh/dot_general | solution.py:56
  404.9 0.8 constant_dynamic-update-slice_fusion.2
  405.7 0.6 dynamic_slice.18
  406.9 0.4 iota_compare_fusion.2
  407.3 15.5 %fusion.135 = (f32[8,2,256]{2,1,0:T(2,128)S(1)}, f32[8,2,256,2048]{3,2,1,0:T(8,128)}) fusion(pred[256,2048]{1,0:T(8,128)(4,1)S(1)} %iota_compare_fusion.2, bf16[8,2048,2,64]{1,3,2,0:T(8,128)(2,1)} %get-tuple-element.150, bf16[8,2048,2,1,64]{1,4,2,0,3:T(8,128)(2,1)} %get-tuple-element.149, s32[]{:T(128)S(6)} %select_n.28), kind=kOutput, calls=%fused_computation.5.clone.1 | convolution fusion | flops 1098903552 | bytes 38813700 | tf_op jit(solution)/shard_map/while/body/eval_jaxpr/bqkgh,bskh->bkgqs/dot_general | solution.py:50
  422.7 15.0 %fusion.136 = f32[8,2,256]{2,1,0:T(2,128)S(1)} fusion(f32[8,2,256,2048]{3,2,1,0:T(8,128)} %get-tuple-element.124, f32[8,2,256]{2,1,0:T(2,128)S(1)} %get-tuple-element.125, pred[256,2048]{1,0:T(8,128)(4,1)S(1)} %iota_compare_fusion.2), kind=kLoop, calls=%fused_computation.4.clone.1 | loop fusion | flops 33550336 | bytes 34111488 | tf_op jit(solution)/shard_map/while/body/eval_jaxpr/reduce_sum | solution.py:55
  437.8 16.3 %fusion.137 = bf16[8,2,256,64]{2,3,1,0:T(8,128)(2,1)S(1)} fusion(bf16[8,2048,2,64]{1,3,2,0:T(8,128)(2,1)} %get-tuple-element.151, f32[8,2,256]{2,1,0:T(2,128)S(1)} %fusion.136, f32[8,2,256]{2,1,0:T(2,128)S(1)} %get-tuple-element.125, f32[8,2,256,2048]{3,2,1,0:T(8,128)} %get-tuple-element.124, pred[256,2048]{1,0:T(8,128)(4,1)S(1)} %iota_compare_fusion.2), kind=kOutput, calls=%fused_computation.9.clone.1 | convolution fusion | flops 1115947008 | bytes 38830080 | tf_op jit(solution)/shard_map/while/body/eval_jaxpr/bkgqs,bskh->bqkgh/dot_general | solution.py:56
  454.1 0.8 constant_dynamic-update-slice_fusion.2
  454.9 0.6 dynamic_slice.18
  456.4 15.5 %fusion.135 = (f32[8,2,256]{2,1,0:T(2,128)S(1)}, f32[8,2,256,2048]{3,2,1,0:T(8,128)}) fusion(pred[256,2048]{1,0:T(8,128)(4,1)S(1)} %iota_compare_fusion.2, bf16[8,2048,2,64]{1,3,2,0:T(8,128)(2,1)} %get-tuple-element.150, bf16[8,2048,2,1,64]{1,4,2,0,3:T(8,128)(2,1)} %get-tuple-element.149, s32[]{:T(128)S(6)} %select_n.28), kind=kOutput, calls=%fused_computation.5.clone.1 | convolution fusion | flops 1098903552 | bytes 38813700 | tf_op jit(solution)/shard_map/while/body/eval_jaxpr/bqkgh,bskh->bkgqs/dot_general | solution.py:50
  471.9 15.0 %fusion.136 = f32[8,2,256]{2,1,0:T(2,128)S(1)} fusion(f32[8,2,256,2048]{3,2,1,0:T(8,128)} %get-tuple-element.124, f32[8,2,256]{2,1,0:T(2,128)S(1)} %get-tuple-element.125, pred[256,2048]{1,0:T(8,128)(4,1)S(1)} %iota_compare_fusion.2), kind=kLoop, calls=%fused_computation.4.clone.1 | loop fusion | flops 33550336 | bytes 34111488 | tf_op jit(solution)/shard_map/while/body/eval_jaxpr/reduce_sum | solution.py:55
  486.9 16.3 %fusion.137 = bf16[8,2,256,64]{2,3,1,0:T(8,128)(2,1)S(1)} fusion(bf16[8,2048,2,64]{1,3,2,0:T(8,128)(2,1)} %get-tuple-element.151, f32[8,2,256]{2,1,0:T(2,128)S(1)} %fusion.136, f32[8,2,256]{2,1,0:T(2,128)S(1)} %get-tuple-element.125, f32[8,2,256,2048]{3,2,1,0:T(8,128)} %get-tuple-element.124, pred[256,2048]{1,0:T(8,128)(4,1)S(1)} %iota_compare_fusion.2), kind=kOutput, calls=%fused_computation.9.clone.1 | convolution fusion | flops 1115947008 | bytes 38830080 | tf_op jit(solution)/shard_map/while/body/eval_jaxpr/bkgqs,bskh->bqkgh/dot_general | solution.py:56
  503.2 0.8 constant_dynamic-update-slice_fusion.2
  504.1 0.6 dynamic_slice.18
  505.6 15.5 %fusion.135 = (f32[8,2,256]{2,1,0:T(2,128)S(1)}, f32[8,2,256,2048]{3,2,1,0:T(8,128)}) fusion(pred[256,2048]{1,0:T(8,128)(4,1)S(1)} %iota_compare_fusion.2, bf16[8,2048,2,64]{1,3,2,0:T(8,128)(2,1)} %get-tuple-element.150, bf16[8,2048,2,1,64]{1,4,2,0,3:T(8,128)(2,1)} %get-tuple-element.149, s32[]{:T(128)S(6)} %select_n.28), kind=kOutput, calls=%fused_computation.5.clone.1 | convolution fusion | flops 1098903552 | bytes 38813700 | tf_op jit(solution)/shard_map/while/body/eval_jaxpr/bqkgh,bskh->bkgqs/dot_general | solution.py:50
  521.1 15.0 %fusion.136 = f32[8,2,256]{2,1,0:T(2,128)S(1)} fusion(f32[8,2,256,2048]{3,2,1,0:T(8,128)} %get-tuple-element.124, f32[8,2,256]{2,1,0:T(2,128)S(1)} %get-tuple-element.125, pred[256,2048]{1,0:T(8,128)(4,1)S(1)} %iota_compare_fusion.2), kind=kLoop, calls=%fused_computation.4.clone.1 | loop fusion | flops 33550336 | bytes 34111488 | tf_op jit(solution)/shard_map/while/body/eval_jaxpr/reduce_sum | solution.py:55
  536.1 16.3 %fusion.137 = bf16[8,2,256,64]{2,3,1,0:T(8,128)(2,1)S(1)} fusion(bf16[8,2048,2,64]{1,3,2,0:T(8,128)(2,1)} %get-tuple-element.151, f32[8,2,256]{2,1,0:T(2,128)S(1)} %fusion.136, f32[8,2,256]{2,1,0:T(2,128)S(1)} %get-tuple-element.125, f32[8,2,256,2048]{3,2,1,0:T(8,128)} %get-tuple-element.124, pred[256,2048]{1,0:T(8,128)(4,1)S(1)} %iota_compare_fusion.2), kind=kOutput, calls=%fused_computation.9.clone.1 | convolution fusion | flops 1115947008 | bytes 38830080 | tf_op jit(solution)/shard_map/while/body/eval_jaxpr/bkgqs,bskh->bqkgh/dot_general | solution.py:56
  552.4 0.8 constant_dynamic-update-slice_fusion.2
  553.2 0.6 dynamic_slice.18
  554.4 0.4 iota_compare_fusion.2
  554.8 15.5 %fusion.135 = (f32[8,2,256]{2,1,0:T(2,128)S(1)}, f32[8,2,256,2048]{3,2,1,0:T(8,128)}) fusion(pred[256,2048]{1,0:T(8,128)(4,1)S(1)} %iota_compare_fusion.2, bf16[8,2048,2,64]{1,3,2,0:T(8,128)(2,1)} %get-tuple-element.150, bf16[8,2048,2,1,64]{1,4,2,0,3:T(8,128)(2,1)} %get-tuple-element.149, s32[]{:T(128)S(6)} %select_n.28), kind=kOutput, calls=%fused_computation.5.clone.1 | convolution fusion | flops 1098903552 | bytes 38813700 | tf_op jit(solution)/shard_map/while/body/eval_jaxpr/bqkgh,bskh->bkgqs/dot_general | solution.py:50
  570.3 15.0 %fusion.136 = f32[8,2,256]{2,1,0:T(2,128)S(1)} fusion(f32[8,2,256,2048]{3,2,1,0:T(8,128)} %get-tuple-element.124, f32[8,2,256]{2,1,0:T(2,128)S(1)} %get-tuple-element.125, pred[256,2048]{1,0:T(8,128)(4,1)S(1)} %iota_compare_fusion.2), kind=kLoop, calls=%fused_computation.4.clone.1 | loop fusion | flops 33550336 | bytes 34111488 | tf_op jit(solution)/shard_map/while/body/eval_jaxpr/reduce_sum | solution.py:55
  585.3 16.3 %fusion.137 = bf16[8,2,256,64]{2,3,1,0:T(8,128)(2,1)S(1)} fusion(bf16[8,2048,2,64]{1,3,2,0:T(8,128)(2,1)} %get-tuple-element.151, f32[8,2,256]{2,1,0:T(2,128)S(1)} %fusion.136, f32[8,2,256]{2,1,0:T(2,128)S(1)} %get-tuple-element.125, f32[8,2,256,2048]{3,2,1,0:T(8,128)} %get-tuple-element.124, pred[256,2048]{1,0:T(8,128)(4,1)S(1)} %iota_compare_fusion.2), kind=kOutput, calls=%fused_computation.9.clone.1 | convolution fusion | flops 1115947008 | bytes 38830080 | tf_op jit(solution)/shard_map/while/body/eval_jaxpr/bkgqs,bskh->bqkgh/dot_general | solution.py:56
  601.6 0.8 constant_dynamic-update-slice_fusion.2
  602.4 0.6 dynamic_slice.18
  603.9 15.5 %fusion.135 = (f32[8,2,256]{2,1,0:T(2,128)S(1)}, f32[8,2,256,2048]{3,2,1,0:T(8,128)}) fusion(pred[256,2048]{1,0:T(8,128)(4,1)S(1)} %iota_compare_fusion.2, bf16[8,2048,2,64]{1,3,2,0:T(8,128)(2,1)} %get-tuple-element.150, bf16[8,2048,2,1,64]{1,4,2,0,3:T(8,128)(2,1)} %get-tuple-element.149, s32[]{:T(128)S(6)} %select_n.28), kind=kOutput, calls=%fused_computation.5.clone.1 | convolution fusion | flops 1098903552 | bytes 38813700 | tf_op jit(solution)/shard_map/while/body/eval_jaxpr/bqkgh,bskh->bkgqs/dot_general | solution.py:50
  619.4 15.0 %fusion.136 = f32[8,2,256]{2,1,0:T(2,128)S(1)} fusion(f32[8,2,256,2048]{3,2,1,0:T(8,128)} %get-tuple-element.124, f32[8,2,256]{2,1,0:T(2,128)S(1)} %get-tuple-element.125, pred[256,2048]{1,0:T(8,128)(4,1)S(1)} %iota_compare_fusion.2), kind=kLoop, calls=%fused_computation.4.clone.1 | loop fusion | flops 33550336 | bytes 34111488 | tf_op jit(solution)/shard_map/while/body/eval_jaxpr/reduce_sum | solution.py:55
  634.4 16.3 %fusion.137 = bf16[8,2,256,64]{2,3,1,0:T(8,128)(2,1)S(1)} fusion(bf16[8,2048,2,64]{1,3,2,0:T(8,128)(2,1)} %get-tuple-element.151, f32[8,2,256]{2,1,0:T(2,128)S(1)} %fusion.136, f32[8,2,256]{2,1,0:T(2,128)S(1)} %get-tuple-element.125, f32[8,2,256,2048]{3,2,1,0:T(8,128)} %get-tuple-element.124, pred[256,2048]{1,0:T(8,128)(4,1)S(1)} %iota_compare_fusion.2), kind=kOutput, calls=%fused_computation.9.clone.1 | convolution fusion | flops 1115947008 | bytes 38830080 | tf_op jit(solution)/shard_map/while/body/eval_jaxpr/bkgqs,bskh->bqkgh/dot_general | solution.py:56
  650.8 0.8 constant_dynamic-update-slice_fusion.2
  651.6 25.8 %convolution_bitcast_fusion = f32[8,8,256,1024]{3,2,0,1:T(8,128)} fusion(bf16[8,8,256,128]{2,3,1,0:T(8,128)(2,1)} %get-tuple-element.42, bf16[128,1024]{1,0:T(8,128)(2,1)S(1)} %copy-done.2), kind=kOutput, calls=%fused_computation.43 | convolution fusion | flops 4294967296 | bytes 71565312 | tf_op jit(solution)/shard_map/nbqc,cd->bnqd/dot_general | solution.py:60
  677.4 43.8 %copy.15 = f32[8,8,256,1024]{3,2,1,0:T(8,128)} copy(f32[8,8,256,1024]{3,2,0,1:T(8,128)} %convolution_bitcast_fusion) | data formatting | bytes 134217728 | tf_op jit(solution)/shard_map/nbqc,cd->bnqd/transpose | solution.py:60
  721.2 37.5 %fusion.73 = (u8[2048,512]{1,0:T(8,128)(4,1)S(1)}, u8[2048,512]{1,0:T(8,128)(4,1)}, f32[8,2048,512]{2,1,0:T(8,128)}) fusion(bf16[8,2048,1024]{2,1,0:T(8,128)(2,1)} %all-gather.5.cloned.1.call-done, bf16[1024,512]{1,0:T(8,128)(2,1)S(1)} %copy-done.3), kind=kOutput, calls=%fused_computation.95 | convolution fusion | flops 17286823936 | bytes 70254592 | tf_op jit(solution)/shard_map/bsd,df->bsf/dot_general | solution.py:71
  758.7 94.3 %bitcast_add_fusion = f32[8,2048,1024]{2,1,0:T(8,128)} fusion(f32[8,8,256,1024]{3,2,1,0:T(8,128)} %copy.15, f32[8,2048,512]{2,1,0:T(8,128)} %get-tuple-element.84, u8[2048,512]{1,0:T(8,128)(4,1)} %get-tuple-element.58, u8[2048,512]{1,0:T(8,128)(4,1)S(1)} %get-tuple-element.57, bf16[512,1024]{1,0:T(8,128)(2,1)S(1)} %copy-done), kind=kOutput, calls=%fused_computation.18 | convolution fusion | flops 17783848960 | bytes 170917888 | tf_op jit(solution)/shard_map/bsf,fd->bsd/dot_general | solution.py:73
  853.0 325.0 %reduce-scatter.2.cloned.1.call-done = f32[8,256,1024]{2,1,0:T(8,128)} async-done(((f32[8,2048,1024]{2,1,0:T(8,128)}), f32[8,256,1024]{2,1,0:T(8,128)}) %reduce-scatter.2.cloned.1.call-update) | async-done | bytes 8388624 | tf_op jit(solution)/shard_map/reduce_scatter | solution.py:74
  1178.0 8.2 fusion.67
  (39 shorter events, 2.0 us)
Async XLA Ops:
  6.5 752.1 %copy-start = (bf16[512,1024]{1,0:T(8,128)(2,1)S(1)}, bf16[512,1024]{1,0:T(8,128)(2,1)}, u32[]{:S(2)}) copy-start(bf16[512,1024]{1,0:T(8,128)(2,1)} %param.20) | copy-start | bytes 3145732
  6.6 170.8 %all-gather.3.cloned.1.call-start = ((), (), s32[]{:S(2)}) async-start(), calls=%async_computation.1 | async-start | bytes 37748736 | tf_op jit(solution)/shard_map/all_gather | solution.py:68
  19.0 702.2 %all-gather.5.cloned.1.call-start = ((), (), s32[]{:S(2)}) async-start(), calls=%async_computation.2 | async-start | bytes 37748736 | tf_op jit(solution)/shard_map/all_gather | solution.py:69
  19.8 1158.2 %reduce-scatter.2.cloned.1.call-start = ((), (), s32[]{:S(2)}) async-start(), calls=%async_computation.3 | async-start | bytes 75497472 | tf_op jit(solution)/shard_map/reduce_scatter | solution.py:74
  223.5 22.7 %slice-start = ((s8[12582912]{0:T(1024)(128)(4,1)}), s8[4194304]{0:T(1024)(128)(4,1)S(1)}, s32[]{:S(2)}) async-start(s8[12582912]{0:T(1024)(128)(4,1)} %bitcast.107), calls=%async_computation.4 | async-start | bytes 8388608
  223.5 22.7 %slice-start.1 = ((s8[12582912]{0:T(1024)(128)(4,1)}), s8[4194304]{0:T(1024)(128)(4,1)S(1)}, s32[]{:S(2)}) async-start(s8[12582912]{0:T(1024)(128)(4,1)} %bitcast.107), calls=%async_computation.5 | async-start | bytes 8388608
  234.0 12.3 %slice-start.2 = ((s8[12582912]{0:T(1024)(128)(4,1)}), s8[4194304]{0:T(1024)(128)(4,1)S(1)}, s32[]{:S(2)}) async-start(s8[12582912]{0:T(1024)(128)(4,1)} %bitcast.107), calls=%async_computation.6 | async-start | bytes 8388608
  258.2 393.4 %copy-start.2 = (bf16[128,1024]{1,0:T(8,128)(2,1)S(1)}, bf16[128,1024]{1,0:T(8,128)(2,1)}, u32[]{:S(2)}) copy-start(bf16[128,1024]{1,0:T(8,128)(2,1)} %param.18) | copy-start | bytes 786436
  677.4 43.8 %copy-start.3 = (bf16[1024,512]{1,0:T(8,128)(2,1)S(1)}, bf16[1024,512]{1,0:T(8,128)(2,1)}, u32[]{:S(2)}) copy-start(bf16[1024,512]{1,0:T(8,128)(2,1)} %param.19) | copy-start | bytes 3145732
  853.0 333.2 %copy-start.1 = (bf16[512,1024]{1,0:T(8,128)(2,1)S(1)}, bf16[512,1024]{1,0:T(8,128)(2,1)}, u32[]{:S(2)}) copy-start(bf16[512,1024]{1,0:T(8,128)(2,1)} %param.20) | copy-start | bytes 3145732
Sparse Core Ops, SparseCore 0:
  19.1 158.1 all-gather.2
  179.0 154.5 all-gather.4
  853.2 324.7 reduce-scatter.1
where the time goes:
time: 1200 us; the launch traced here: 1190 us
  waiting for transfers between devices  480 us (40%)
  matrix products  458 us (38%)
  other arithmetic  182 us (15%)
  local copies, waits for them, and re-layouts  55.1 us (5%)
  between operations  13.4 us (1%)
    reduce_scatter x1, waiting for transfers between devices, local_layer(): lax.psum_scatter(attn_part + mlp_part, 'tp', scatter_dimension=1, tiled=T...  325 us
    all_gather x1, waiting for transfers between devices, local_layer(): attn_in = lax.all_gather(normed_attn, 'tp', axis=1, tiled=True)  154 us
    dot_general x8, matrix products, one_block(): jnp.einsum('bkgqs,bskh->bqkgh', attn_probs, value_seq, preferred_element_...  130 us
    dot_general x8, matrix products, one_block(): jnp.einsum('bqkgh,bskh->bkgqs', query_blk, key_rot, preferred_element_typ...  124 us
    reduce_sum x8, other arithmetic, one_block(): jnp.sum(exp_scores, axis=-1, keepdims=True)  120 us
    dot_general x1, matrix products, local_layer(): jnp.einsum('bsf,fd->bsd', up_act, w_down_part, preferred_element_type=jnp...  94.3 us
    dot_general x1, matrix products, attention_branch(): jnp.einsum('bsd,dkc->bskc', normed, w_qkv_part, preferred_element_type=jn...  46.2 us
    transpose x1, local copies, waits for them, and re-layouts, attention_branch(): jnp.einsum('nbqc,cd->bnqd', ctx_blocks, w_out_part, preferred_element_typ...  43.8 us
  transfers between devices with their start and end apart: 3, of which 2 were waited for; matrix products, arithmetic and copies ran while one was open for 45% of the time, Pallas kernels for 0%

commit v1 on v0

v1 whole, which is shorter than its diff:
```python
import functools

import jax
import jax.numpy as jnp
from jax import lax
from jax.experimental import pallas as pl
from jax.experimental.pallas import tpu as pltpu
from jax.sharding import PartitionSpec as P

BF16 = jnp.bfloat16
F32 = jnp.float32
VMEM_LIMIT = 60 * 1024 * 1024


def norm_rows(rows, gain, bias):
    rows32 = rows.astype(F32)
    mean = jnp.mean(rows32, axis=-1, keepdims=True)
    centered = rows32 - mean
    var = jnp.mean(centered * centered, axis=-1, keepdims=True)
    return (centered * lax.rsqrt(var + 1e-5) * gain + bias).astype(BF16)


def swap_halves(vals, lane_mod, half):
    width = vals.shape[-1]
    return jnp.where(lane_mod < half, pltpu.roll(vals, width - half, 1), pltpu.roll(vals, half, 1))


def qkv_kernel(head_dim, x_ref, w_ref, cos_ref, sin_ref, gain_ref, bias_ref, q_ref, k_ref, v_ref):
    blocks, rows, width = x_ref.shape
    normed = norm_rows(x_ref[...].reshape(blocks * rows, width), gain_ref[...], bias_ref[...])
    pair = q_ref.shape[2]
    cos_tab, sin_tab = cos_ref[...], sin_ref[...]
    lane_mod = lax.broadcasted_iota(jnp.int32, cos_tab.shape, 1) % head_dim
    scale = head_dim ** -0.5

    def rotate(vals):
        vals = vals.astype(BF16).astype(F32)
        return (vals * cos_tab + swap_halves(vals, lane_mod, head_dim // 2) * sin_tab).astype(BF16)

    for p in range(w_ref.shape[0]):
        qkv = jnp.dot(normed, w_ref[p], preferred_element_type=F32)
        q_ref[p] = (rotate(qkv[:, :pair]).astype(F32) * scale).astype(BF16)
        k_ref[p] = rotate(qkv[:, pair:2 * pair]).astype(F32).T.astype(BF16)
        v_ref[p] = qkv[:, 2 * pair:].astype(BF16)


def attn_kernel(head_dim, q_ref, k_ref, v_ref, o_ref, s_ref):
    block = q_ref.shape[1]
    pair = q_ref.shape[2]
    heads = pair // head_dim
    num_blocks = k_ref.shape[2] // block

    def one_block(i):
        q = q_ref[0]
        lane = lax.broadcasted_iota(jnp.int32, q.shape, 1)
        zero = jnp.zeros_like(q)
        q_all = jnp.concatenate([jnp.where(lane // head_dim == h, q, zero) for h in range(heads)], axis=0)
        m = None
        for c in range(i + 1):
            s = jnp.dot(q_all, k_ref[0, :, c * block:(c + 1) * block], preferred_element_type=F32)
            if c == i:
                row = lax.broadcasted_iota(jnp.int32, s.shape, 0) % block
                col = lax.broadcasted_iota(jnp.int32, s.shape, 1)
                s = jnp.where(col <= row, s, -1e30)
            s_ref[:, c * block:(c + 1) * block] = s
            part = functools.reduce(jnp.maximum, [s[:, t:t + 128] for t in range(0, block, 128)])
            m = part if m is None else jnp.maximum(m, part)
        m = jnp.max(m, axis=1, keepdims=True)
        total, acc = None, None
        for c in range(i + 1):
            e = jnp.exp(s_ref[:, c * block:(c + 1) * block] - m)
            part = functools.reduce(jnp.add, [e[:, t:t + 128] for t in range(0, block, 128)])
            total = part if total is None else total + part
            pv = jnp.dot(e.astype(BF16), v_ref[0, c * block:(c + 1) * block, :], preferred_element_type=F32)
            acc = pv if acc is None else acc + pv
        out = acc / jnp.sum(total, axis=1, keepdims=True)
        lane_out = lax.broadcasted_iota(jnp.int32, (block, pair), 1)
        res = out[:block]
        for h in range(1, heads):
            res = jnp.where(lane_out // head_dim == h, out[h * block:(h + 1) * block], res)
        o_ref[...] = res.astype(BF16)

    for i in range(num_blocks):
        pl.when(pl.program_id(1) == i)(functools.partial(one_block, i))


def mlp_kernel(x_ref, gain_ref, bias_ref, up_ref, down_ref, o_ref, m_ref, acc_ref):
    f, t = pl.program_id(0), pl.program_id(1)
    rows = x_ref.shape[0]
    sl = pl.ds(pl.multiple_of(t * rows, rows), rows)

    @pl.when(f == 0)
    def _():
        m_ref[sl, :] = norm_rows(x_ref[...], gain_ref[...], bias_ref[...])

    half = rows // 2
    for h in range(2):
        part = pl.ds(pl.multiple_of(t * rows + h * half, half), half)
        pre = jnp.dot(m_ref[part, :], up_ref[0], preferred_element_type=F32)
        act = (0.5 * pre * (1.0 + lax.erf(pre * (0.5 ** 0.5)))).astype(BF16)
        down = jnp.dot(act, down_ref[0], preferred_element_type=F32)

        @pl.when(f == 0)
        def _(part=part, down=down):
            acc_ref[part, :] = down

        @pl.when(f > 0)
        def _(part=part, down=down):
            acc_ref[part, :] += down

    @pl.when(f == pl.num_programs(0) - 1)
    def _():
        o_ref[...] = acc_ref[sl, :]


def final_kernel(x_ref, ctx_ref, wo_ref, mlp_ref, y_ref):
    attn = jnp.dot(ctx_ref[...], wo_ref[...], preferred_element_type=F32)
    y_ref[...] = (x_ref[...].astype(F32) + attn + mlp_ref[...]).astype(BF16)


def params(sem):
    return pltpu.CompilerParams(dimension_semantics=sem, vmem_limit_bytes=VMEM_LIMIT)


def solution(mesh):
    tp = mesh.shape['tp']

    def local_layer(x, attn_gain, attn_bias, mlp_gain, mlp_bias, w_qkv, w_out, w_up, w_down, positions):
        batch, chunk, width = x.shape
        per_dev = batch // tp
        groups, slot_cols = w_qkv.shape[1:]
        ctx_cols = w_out.shape[0]
        head_dim = (slot_cols - ctx_cols // groups) // 2
        pair = groups * head_dim
        seq = chunk * tp
        ff = w_up.shape[1]
        tokens = batch * chunk
        half = head_dim // 2

        w_qkv = w_qkv.reshape(width, groups, 3, head_dim).swapaxes(1, 2).reshape(width, 3 * pair)
        wqkv_all = lax.all_gather(w_qkv, 'tp', axis=0, tiled=False)
        x_seq = lax.all_to_all(x, 'tp', split_axis=0, concat_axis=0, tiled=True)
        x_seq = x_seq.reshape(tp, chunk, width)

        inv_freq = 10000.0 ** (-2.0 * jnp.arange(half, dtype=F32) / head_dim)
        inv_freq = jnp.tile(inv_freq, 2 * groups)
        angles = positions.astype(F32)[:, None] * inv_freq[None, :]
        sign = jnp.where(jnp.arange(pair) % head_dim < half, -1.0, 1.0).astype(F32)
        cos_tab, sin_tab = jnp.cos(angles), jnp.sin(angles) * sign[None, :]

        gain2, bias2 = attn_gain.reshape(1, width), attn_bias.reshape(1, width)
        nb = 2
        q, k, v = pl.pallas_call(
            functools.partial(qkv_kernel, head_dim),
            grid=(tp // nb,),
            in_specs=[
                pl.BlockSpec((nb, chunk, width), lambda i: (i, 0, 0)),
                pl.BlockSpec((tp, width, 3 * pair), lambda i: (0, 0, 0)),
                pl.BlockSpec((nb * chunk, pair), lambda i: (i, 0)),
                pl.BlockSpec((nb * chunk, pair), lambda i: (i, 0)),
                pl.BlockSpec((1, width), lambda i: (0, 0)),
                pl.BlockSpec((1, width), lambda i: (0, 0)),
            ],
            out_specs=[
                pl.BlockSpec((tp, nb * chunk, pair), lambda i: (0, i, 0)),
                pl.BlockSpec((tp, pair, nb * chunk), lambda i: (0, 0, i)),
                pl.BlockSpec((tp, nb * chunk, pair), lambda i: (0, i, 0)),
            ],
            out_shape=[
                jax.ShapeDtypeStruct((tp, seq, pair), BF16),
                jax.ShapeDtypeStruct((tp, pair, seq), BF16),
                jax.ShapeDtypeStruct((tp, seq, pair), BF16),
            ],
            compiler_params=params(('arbitrary',)),
            cost_estimate=pl.CostEstimate(flops=2 * seq * width * 3 * pair * tp, bytes_accessed=2 * (seq * width * 4 + width * 3 * pair * tp), transcendentals=0),
            name='qkv',
        )(x_seq, wqkv_all, cos_tab, sin_tab, gain2, bias2)

        block = chunk
        ctx = pl.pallas_call(
            functools.partial(attn_kernel, head_dim),
            grid=(tp, seq // block),
            in_specs=[
                pl.BlockSpec((1, block, pair), lambda p, i: (p, i, 0)),
                pl.BlockSpec((1, pair, seq), lambda p, i: (p, 0, 0)),
                pl.BlockSpec((1, seq, pair), lambda p, i: (p, 0, 0)),
            ],
            out_specs=pl.BlockSpec((block, pair), lambda p, i: (i, p)),
            out_shape=jax.ShapeDtypeStruct((seq, tp * pair), BF16),
            scratch_shapes=[pltpu.VMEM((groups * block, seq), F32)],
            compiler_params=params(('arbitrary', 'arbitrary')),
            cost_estimate=pl.CostEstimate(flops=8 * seq * seq * pair * tp, bytes_accessed=2 * seq * width * 4, transcendentals=0),
            name='attn',
        )(q, k, v)

        w_up, w_down, w_out, _, _ = lax.optimization_barrier((w_up, w_down, w_out, wqkv_all, x_seq))
        up_all = lax.all_gather(w_up, 'tp', axis=0, tiled=False)
        down_all = lax.all_gather(w_down, 'tp', axis=0, tiled=False)
        wo_all = lax.all_gather(w_out, 'tp', axis=0, tiled=True)
        x_mlp, ctx = lax.optimization_barrier((x, ctx))
        ctx_own = lax.all_to_all(ctx.reshape(tp, chunk, width), 'tp', split_axis=0, concat_axis=0, tiled=True)
        x_rows = x_mlp.reshape(tokens, width)
        rows = 512
        nt = tokens // rows
        mlp = pl.pallas_call(
            mlp_kernel,
            grid=(tp, nt),
            in_specs=[
                pl.BlockSpec((rows, width), lambda f, t: (jnp.where(f == 0, t, nt - 1), 0)),
                pl.BlockSpec((1, width), lambda f, t: (0, 0)),
                pl.BlockSpec((1, width), lambda f, t: (0, 0)),
                pl.BlockSpec((1, width, ff), lambda f, t: (f, 0, 0)),
                pl.BlockSpec((1, ff, width), lambda f, t: (f, 0, 0)),
            ],
            out_specs=pl.BlockSpec((rows, width), lambda f, t: (jnp.where(f == tp - 1, t, 0), 0)),
            out_shape=jax.ShapeDtypeStruct((tokens, width), F32),
            scratch_shapes=[pltpu.VMEM((tokens, width), BF16), pltpu.VMEM((tokens, width), F32)],
            compiler_params=params(('arbitrary', 'arbitrary')),
            cost_estimate=pl.CostEstimate(flops=4 * tokens * width * ff * tp, bytes_accessed=4 * tokens * width * 2, transcendentals=0),
            name='mlp',
        )(x_rows, mlp_gain.reshape(1, width), mlp_bias.reshape(1, width), up_all, down_all)

        y = pl.pallas_call(
            final_kernel,
            grid=(nt,),
            in_specs=[
                pl.BlockSpec((rows, width), lambda t: (t, 0)),
                pl.BlockSpec((rows, width), lambda t: (t, 0)),
                pl.BlockSpec((width, width), lambda t: (0, 0)),
                pl.BlockSpec((rows, width), lambda t: (t, 0)),
            ],
            out_specs=pl.BlockSpec((rows, width), lambda t: (t, 0)),
            out_shape=jax.ShapeDtypeStruct((tokens, width), BF16),
            compiler_params=params(('arbitrary',)),
            cost_estimate=pl.CostEstimate(flops=2 * tokens * width * width, bytes_accessed=tokens * width * 10, transcendentals=0),
            name='final',
        )(x_rows, ctx_own.reshape(tokens, width), wo_all, mlp)
        return y.reshape(batch, chunk, width)

    return jax.shard_map(local_layer, mesh=mesh, in_specs=(P('dp', 'tp', None), P(), P(), P(), P(), P(None, 'tp', None), P('tp', None), P(None, 'tp'), P('tp', None), P()), out_specs=P('dp', 'tp', None), check_vma=False)
```

time: 1200 us -> 316 us (0.26)
  waiting for transfers between devices: 480 us -> 2.41 us
  matrix products: 458 us -> 0 us
  Pallas kernels: 0 us -> 206 us
  other arithmetic: 182 us -> 5.6 us
  blocking collectives: 0 us -> 80.2 us
  local copies, waits for them, and re-layouts: 55.1 us -> 2.43 us
    dot_general x20 -> x0, matrix products: 458 us -> none  [the longest x8 130 us: one_block(): jnp.einsum('bkgqs,bskh->bqkgh', attn_probs, value_seq, preferred_element_...]
    reduce_scatter x1 -> x0, waiting for transfers between devices: 325 us -> none  [local_layer(): lax.psum_scatter(attn_part + mlp_part, 'tp', scatter_dimension=1, tiled=T...]
    pallas_call x0 -> x4, Pallas kernels: none -> 206 us  [the longest x1 101 us: local_layer(): pl.pallas_call(functools.partial(attn_kernel, head_dim), grid=(tp, seq //...]
    all_gather x2 -> x4, waiting for transfers between devices: 154 us -> 0.99 us  [the longest x1 0.94 us: local_layer(): wqkv_all = lax.all_gather(w_qkv, 'tp', axis=0, tiled=False)]
    reduce_sum x10 -> x0, other arithmetic: 126 us -> none  [the longest x8 120 us: one_block(): jnp.sum(exp_scores, axis=-1, keepdims=True)]
    all_to_all x0 -> x1, blocking collectives: none -> 80.2 us  [local_layer(): x_seq = lax.all_to_all(x, 'tp', split_axis=0, concat_axis=0, tiled=True)]
    transpose x1, local copies, waits for them, and re-layouts: 43.8 us -> 1.19 us  [local_layer(): w_qkv.reshape(width, groups, 3, head_dim).swapaxes(1, 2)]
    convert_element_type x5 -> x1, other arithmetic: 27.3 us -> 0.01 us  [local_layer(): angles = positions.astype(F32)[:, None] * inv_freq[None, :]]
  transfers between devices with their start and end apart: 3 -> 5, of which waited for: 2 -> 1; matrix products, arithmetic and copies ran while one was open for 45% -> 2% of each run, Pallas kernels for 0% -> 62%
where the time goes in v1:
time: 316 us; the launch traced here: 315 us
  Pallas kernels  206 us (65%)
  blocking collectives  80.2 us (25%)
  between operations  13.2 us (4%)
  other arithmetic  5.6 us (2%)
  starting transfers between devices  4.88 us (2%)
    pallas_call x1, Pallas kernels, local_layer(): pl.pallas_call(functools.partial(attn_kernel, head_dim), grid=(tp, seq //...  101 us
    all_to_all x1, blocking collectives, local_layer(): x_seq = lax.all_to_all(x, 'tp', split_axis=0, concat_axis=0, tiled=True)  80.2 us
    pallas_call x1, Pallas kernels, local_layer(): pl.pallas_call(mlp_kernel, grid=(tp, nt), in_specs=[pl.BlockSpec((rows, w...  67.6 us
    pallas_call x1, Pallas kernels, local_layer(): pl.pallas_call(functools.partial(qkv_kernel, head_dim), grid=(tp // nb,),...  26 us
    pallas_call x1, Pallas kernels, local_layer(): pl.pallas_call(final_kernel, grid=(nt,), in_specs=[pl.BlockSpec((rows, wi...  11.4 us
  transfers between devices with their start and end apart: 5, of which 1 were waited for; matrix products, arithmetic and copies ran while one was open for 2% of the time, Pallas kernels for 62%

profile of v1, /device:TPU:81, one launch (start us, length us, event | category | flops | bytes accessed | tf_op | source)
XLA Modules:
  0.0 314.6 jit_solution(10419515246817574599)
XLA Ops:
  6.5 0.0 all-gather.7.cloned.1.call-start
  6.6 1.2 copy.15
  7.7 1.2 copy.16
  8.9 0.1 all-gather.7.cloned.1.call-update
  9.0 0.0 copy-start
  9.0 0.1 all-gather.11.cloned.1.call-start
  9.0 80.2 %all_to_all.10.x_ref = bf16[8,256,1024]{2,1,0:T(8,128)(2,1)} all-to-all(bf16[8,256,1024]{2,1,0:T(8,128)(2,1)} %param.10), channel_id=1, replica_groups=mesh['dp'=4,'tp'=8] {'tp'}, dimensions={0} | all-to-all | bytes 8388608 | tf_op jit(solution)/shard_map/all_to_all | solution.py:142
  89.2 0.9 all-gather.7.cloned.1.call-done.w_ref
  90.2 0.1 all-gather.11.cloned.1.call-update
  90.3 0.1 all-gather.13.cloned.1.call-start
  90.3 0.7 all-gather.13.cloned.1.call-update
  91.0 0.0 copy-done
  91.1 0.1 mul.27
  91.2 5.6 %fusion = (f32[2048,128]{1,0:T(8,128)}, f32[2048,128]{1,0:T(8,128)}) fusion(f32[128]{0:T(128)S(1)} %compare_select_fusion, f32[128]{0:T(128)S(1)} %mul.27, f32[2048]{0:T(1024)S(1)} %convert_element_type.3), kind=kLoop, calls=%fused_computation.2 | loop fusion | flops 524288 | bytes 2106368 | tf_op jit(solution)/shard_map/mul | solution.py:149
  96.8 26.0 %qkv.1 = (bf16[8,2048,128]{2,1,0:T(8,128)(2,1)}, bf16[8,128,2048]{2,1,0:T(8,128)(2,1)}, bf16[8,2048,128]{2,1,0:T(8,128)(2,1)}) custom-call(bf16[8,256,1024]{2,1,0:T(8,128)(2,1)} %all_to_all.10.x_ref, bf16[8,1024,384]{2,1,0:T(8,128)(2,1)} %all-gather.7.cloned.1.call-done.w_ref, f32[2048,128]{1,0:T(8,128)} %get-tuple-element.22.cos_ref, ...), custom_call_target="tpu_custom_call" | custom-call | flops 12884901888 | bytes 23068672 | tf_op jit(solution)/shard_map/qkv/pallas_call | solution.py:153
  122.8 100.9 %attn.1 = bf16[2048,1024]{1,0:T(8,128)(2,1)} custom-call(bf16[8,2048,128]{2,1,0:T(8,128)(2,1)} %get-tuple-element.13.q_ref, bf16[8,128,2048]{2,1,0:T(8,128)(2,1)} %get-tuple-element.14.k_ref, bf16[8,2048,128]{2,1,0:T(8,128)(2,1)} %get-tuple-element.15.v_ref), custom_call_target="tpu_custom_call" | custom-call | flops 34359738368 | bytes 16777216 | tf_op jit(solution)/shard_map/attn/pallas_call | solution.py:180
  223.7 4.7 %all-to-all-start.1 = ((bf16[8,256,1024]{2,1,0:T(8,128)(2,1)}), bf16[8,256,1024]{2,1,0:T(8,128)(2,1)}, u32[]{:S(2)}, u32[]{:S(2)}) async-start(bf16[8,256,1024]{2,1,0:T(8,128)(2,1)} %bitcast.16), calls=%async_computation.1 | async-start | bytes 8388608 | tf_op jit(solution)/shard_map/all_to_all | solution.py:201
  228.4 0.0 all-gather.9.cloned.1.call-start
  228.4 0.6 all-gather.9.cloned.1.call-update
  229.0 0.0 all-gather.11.cloned.1.call-done
  229.0 0.0 all-gather.13.cloned.1.call-done
  229.1 67.6 %mlp.1.mlp_ref = f32[2048,1024]{1,0:T(8,128)} custom-call(bf16[2048,1024]{1,0:T(8,128)(2,1)} %bitcast.14, f32[1,1024]{1,0:T(1,128)} %bitcast.23, f32[1,1024]{1,0:T(1,128)} %bitcast.24, bf16[8,1024,512]{2,1,0:T(8,128)(2,1)} %bitcast.19, bf16[8,512,1024]{2,1,0:T(8,128)(2,1)} %bitcast.20), custom_call_target="tpu_custom_call" | custom-call | flops 34359738368 | bytes 16777216 | tf_op jit(solution)/shard_map/mlp/pallas_call | solution.py:205
  296.7 0.0 all-to-all-done.1
  296.7 0.0 all-gather.9.cloned.1.call-done.wo_ref
  296.7 11.4 %final.1 = bf16[2048,1024]{1,0:T(8,128)(2,1)} custom-call(bf16[2048,1024]{1,0:T(8,128)(2,1)} %bitcast.15, bf16[2048,1024]{1,0:T(8,128)(2,1)} %bitcast.7.ctx_ref, bf16[1024,1024]{1,0:T(8,128)(2,1)} %all-gather.9.cloned.1.call-done.wo_ref, f32[2048,1024]{1,0:T(8,128)} %mlp.1.mlp_ref), custom_call_target="tpu_custom_call" | custom-call | flops 4294967296 | bytes 20971520 | tf_op jit(solution)/shard_map/final/pallas_call | solution.py:223
  (4 shorter events, 0.0 us)
Async XLA Ops:
  6.5 83.6 %all-gather.7.cloned.1.call-start = ((), (), s32[]{:S(2)}) async-start(), calls=%async_computation.2 | async-start | bytes 7077888 | tf_op jit(solution)/shard_map/all_gather | solution.py:141
  9.0 82.1 %copy-start = (s32[2048]{0:T(1024)S(1)}, s32[2048]{0:T(1024)}, u32[]{:S(2)}) copy-start(s32[2048]{0:T(1024)} %param.19) | copy-start | bytes 24580
  9.0 220.1 %all-gather.11.cloned.1.call-start = ((), (), s32[]{:S(2)}) async-start(), calls=%async_computation.4 | async-start | bytes 9437184 | tf_op jit(solution)/shard_map/all_gather | solution.py:197
  90.3 138.8 %all-gather.13.cloned.1.call-start = ((), (), s32[]{:S(2)}) async-start(), calls=%async_computation.5 | async-start | bytes 9437184 | tf_op jit(solution)/shard_map/all_gather | solution.py:198
  223.7 73.0 %all-to-all-start.1 = ((bf16[8,256,1024]{2,1,0:T(8,128)(2,1)}), bf16[8,256,1024]{2,1,0:T(8,128)(2,1)}, u32[]{:S(2)}, u32[]{:S(2)}) async-start(bf16[8,256,1024]{2,1,0:T(8,128)(2,1)} %bitcast.16), calls=%async_computation.1 | async-start | bytes 8388608 | tf_op jit(solution)/shard_map/all_to_all | solution.py:201
  228.4 68.3 %all-gather.9.cloned.1.call-start = ((), (), s32[]{:S(2)}) async-start(), calls=%async_computation.3 | async-start | bytes 2359296 | tf_op jit(solution)/shard_map/all_gather | solution.py:199
Sparse Core Ops, SparseCore 0:
  9.1 81.0 all-gather.6
  91.8 48.0 all-gather.10
  141.5 46.6 all-gather.12
  230.5 31.8 all-gather.8

commit v2 on v1

--- a/solution.py
+++ b/solution.py
@@ -37,80 +37,106 @@
         vals = vals.astype(BF16).astype(F32)
         return (vals * cos_tab + swap_halves(vals, lane_mod, head_dim // 2) * sin_tab).astype(BF16)
 
-    for p in range(w_ref.shape[0]):
-        qkv = jnp.dot(normed, w_ref[p], preferred_element_type=F32)
-        q_ref[p] = (rotate(qkv[:, :pair]).astype(F32) * scale).astype(BF16)
-        k_ref[p] = rotate(qkv[:, pair:2 * pair]).astype(F32).T.astype(BF16)
-        v_ref[p] = qkv[:, 2 * pair:].astype(BF16)
-
-
-def attn_kernel(head_dim, q_ref, k_ref, v_ref, o_ref, s_ref):
-    block = q_ref.shape[1]
-    pair = q_ref.shape[2]
-    heads = pair // head_dim
-    num_blocks = k_ref.shape[2] // block
-
-    def one_block(i):
-        q = q_ref[0]
-        lane = lax.broadcasted_iota(jnp.int32, q.shape, 1)
-        zero = jnp.zeros_like(q)
-        q_all = jnp.concatenate([jnp.where(lane // head_dim == h, q, zero) for h in range(heads)], axis=0)
-        m = None
-        for c in range(i + 1):
-            s = jnp.dot(q_all, k_ref[0, :, c * block:(c + 1) * block], preferred_element_type=F32)
-            if c == i:
-                row = lax.broadcasted_iota(jnp.int32, s.shape, 0) % block
-                col = lax.broadcasted_iota(jnp.int32, s.shape, 1)
-                s = jnp.where(col <= row, s, -1e30)
-            s_ref[:, c * block:(c + 1) * block] = s
-            part = functools.reduce(jnp.maximum, [s[:, t:t + 128] for t in range(0, block, 128)])
-            m = part if m is None else jnp.maximum(m, part)
-        m = jnp.max(m, axis=1, keepdims=True)
-        total, acc = None, None
-        for c in range(i + 1):
-            e = jnp.exp(s_ref[:, c * block:(c + 1) * block] - m)
-            part = functools.reduce(jnp.add, [e[:, t:t + 128] for t in range(0, block, 128)])
-            total = part if total is None else total + part
-            pv = jnp.dot(e.astype(BF16), v_ref[0, c * block:(c + 1) * block, :], preferred_element_type=F32)
-            acc = pv if acc is None else acc + pv
-        out = acc / jnp.sum(total, axis=1, keepdims=True)
-        lane_out = lax.broadcasted_iota(jnp.int32, (block, pair), 1)
-        res = out[:block]
-        for h in range(1, heads):
-            res = jnp.where(lane_out // head_dim == h, out[h * block:(h + 1) * block], res)
-        o_ref[...] = res.astype(BF16)
-
-    for i in range(num_blocks):
-        pl.when(pl.program_id(1) == i)(functools.partial(one_block, i))
-
-
-def mlp_kernel(x_ref, gain_ref, bias_ref, up_ref, down_ref, o_ref, m_ref, acc_ref):
+    for p in range(0, w_ref.shape[0], 2):
+        for h in range(2):
+            qk = jnp.dot(normed, w_ref[p + h, :, :2 * pair], preferred_element_type=F32)
+            q_ref[p + h] = (rotate(qk[:, :pair]).astype(F32) * scale).astype(BF16)
+            k_ref[p + h] = rotate(qk[:, pair:]).astype(F32).T.astype(BF16)
+        w_val = jnp.concatenate([w_ref[p, :, 2 * pair:], w_ref[p + 1, :, 2 * pair:]], axis=1)
+        vals = jnp.dot(normed, w_val, preferred_element_type=F32).astype(BF16)
+        v_ref[p] = vals[:, :pair]
+        v_ref[p + 1] = vals[:, pair:]
+
+
+def attn_kernel(head_dim, rows, chunk, q_ref, k_ref, v_ref, o_ref, s_ref):
+    seq, pair = o_ref.shape
+    units = [(r, h) for r in range(0, seq, rows) for h in range(pair // head_dim)]
+    lane = lax.broadcasted_iota(jnp.int32, (rows, pair), 1)
+
+    def fold(op, vals, carry):
+        for t in range(0, vals.shape[1], 128):
+            part = vals[:, t:t + 128]
+            carry = part if carry is None else op(carry, part)
+        return carry
+
+    def load_query(unit):
+        r, h = unit
+        q = q_ref[0, r:r + rows, :]
+        return jnp.where(lane // head_dim == h, q, jnp.zeros_like(q))
+
+    def scores(unit, buf, q, cols, m):
+        r, (c, size) = unit[0], cols
+        s = jnp.dot(q, k_ref[0, :, c:c + size], preferred_element_type=F32)
+        if c + size > r:
+            row = lax.broadcasted_iota(jnp.int32, s.shape, 0) + r
+            col = lax.broadcasted_iota(jnp.int32, s.shape, 1) + c
+            s = jnp.where(col <= row, s, -1e30)
+        s_ref[buf, :, c:c + size] = s
+        return fold(jnp.maximum, s, m)
+
+    def weigh(buf, m, cols, total, acc):
+        c, size = cols
+        e = jnp.exp(s_ref[buf, :, c:c + size] - m)
+        total = fold(jnp.add, e, total)
+        pv = jnp.dot(e.astype(BF16), v_ref[0, c:c + size, :], preferred_element_type=F32)
+        return total, pv if acc is None else acc + pv
+
+    def starts(unit):
+        end = unit[0] + rows
+        return [(c, min(chunk, end - c)) for c in range(0, end, chunk)]
+
+    q_next, m_next = load_query(units[0]), None
+    for c in starts(units[0]):
+        m_next = scores(units[0], 0, q_next, c, m_next)
+    for n, unit in enumerate(units):
+        m = jnp.max(m_next, axis=1, keepdims=True)
+        total = acc = m_next = None
+        follow = units[n + 1] if n + 1 < len(units) else None
+        todo = starts(follow) if follow else []
+        if follow:
+            q_next = load_query(follow)
+        for j in range(max(len(todo), len(starts(unit)))):
+            if j < len(todo):
+                m_next = scores(follow, (n + 1) % 2, q_next, todo[j], m_next)
+            if j < len(starts(unit)):
+                total, acc = weigh(n % 2, m, starts(unit)[j], total, acc)
+        r, h = unit
+        out = (acc / jnp.sum(total, axis=1, keepdims=True)).astype(BF16)
+        o_ref[r:r + rows, h * head_dim:(h + 1) * head_dim] = out[:, h * head_dim:(h + 1) * head_dim]
+
+
+def mlp_kernel(sub, x_ref, gain_ref, bias_ref, up_ref, down_ref, o_ref, m_ref, acc_ref):
     f, t = pl.program_id(0), pl.program_id(1)
-    rows = x_ref.shape[0]
-    sl = pl.ds(pl.multiple_of(t * rows, rows), rows)
+    rows, width = x_ref.shape
+    shards, ff = up_ref.shape[0], up_ref.shape[2]
+    base = pl.multiple_of(t * rows, rows)
 
     @pl.when(f == 0)
     def _():
-        m_ref[sl, :] = norm_rows(x_ref[...], gain_ref[...], bias_ref[...])
-
-    half = rows // 2
-    for h in range(2):
-        part = pl.ds(pl.multiple_of(t * rows + h * half, half), half)
-        pre = jnp.dot(m_ref[part, :], up_ref[0], preferred_element_type=F32)
-        act = (0.5 * pre * (1.0 + lax.erf(pre * (0.5 ** 0.5)))).astype(BF16)
-        down = jnp.dot(act, down_ref[0], preferred_element_type=F32)
-
-        @pl.when(f == 0)
-        def _(part=part, down=down):
-            acc_ref[part, :] = down
-
-        @pl.when(f > 0)
-        def _(part=part, down=down):
-            acc_ref[part, :] += down
+        for h in range(0, rows, sub):
+            part = pl.ds(base + h, sub)
+            m_ref[part, :] = norm_rows(x_ref[h:h + sub, :], gain_ref[...], bias_ref[...])
+            acc_ref[part, :] = jnp.zeros((sub, width), F32)
+
+    down_w = down_ref[...].reshape(shards * ff, width)
+
+    def expand(h):
+        rows_in = m_ref[pl.ds(base + h, sub), :]
+        return [jnp.dot(rows_in, up_ref[k], preferred_element_type=F32) for k in range(shards)]
+
+    def gelu(pre):
+        return (0.5 * pre * (1.0 + lax.erf(pre * (0.5 ** 0.5)))).astype(BF16)
+
+    pre = expand(0)
+    for h in range(0, rows, sub):
+        following = expand(h + sub) if h + sub < rows else None
+        act = jnp.concatenate([gelu(p) for p in pre], axis=1)
+        acc_ref[pl.ds(base + h, sub), :] += jnp.dot(act, down_w, preferred_element_type=F32)
+        pre = following
 
     @pl.when(f == pl.num_programs(0) - 1)
     def _():
-        o_ref[...] = acc_ref[sl, :]
+        o_ref[...] = acc_ref[pl.ds(base, rows), :]
 
 
 def final_kernel(x_ref, ctx_ref, wo_ref, mlp_ref, y_ref):
@@ -176,19 +202,19 @@
             name='qkv',
         )(x_seq, wqkv_all, cos_tab, sin_tab, gain2, bias2)
 
-        block = chunk
+        q_rows, kv_cols = 256, 512
         ctx = pl.pallas_call(
-            functools.partial(attn_kernel, head_dim),
-            grid=(tp, seq // block),
-            in_specs=[
-                pl.BlockSpec((1, block, pair), lambda p, i: (p, i, 0)),
-                pl.BlockSpec((1, pair, seq), lambda p, i: (p, 0, 0)),
-                pl.BlockSpec((1, seq, pair), lambda p, i: (p, 0, 0)),
-            ],
-            out_specs=pl.BlockSpec((block, pair), lambda p, i: (i, p)),
+            functools.partial(attn_kernel, head_dim, q_rows, kv_cols),
+            grid=(tp,),
+            in_specs=[
+                pl.BlockSpec((1, seq, pair), lambda p: (p, 0, 0)),
+                pl.BlockSpec((1, pair, seq), lambda p: (p, 0, 0)),
+                pl.BlockSpec((1, seq, pair), lambda p: (p, 0, 0)),
+            ],
+            out_specs=pl.BlockSpec((seq, pair), lambda p: (0, p)),
             out_shape=jax.ShapeDtypeStruct((seq, tp * pair), BF16),
-            scratch_shapes=[pltpu.VMEM((groups * block, seq), F32)],
-            compiler_params=params(('arbitrary', 'arbitrary')),
+            scratch_shapes=[pltpu.VMEM((2, q_rows, seq), F32)],
+            compiler_params=params(('arbitrary',)),
             cost_estimate=pl.CostEstimate(flops=8 * seq * seq * pair * tp, bytes_accessed=2 * seq * width * 4, transcendentals=0),
             name='attn',
         )(q, k, v)
@@ -200,19 +226,19 @@
         x_mlp, ctx = lax.optimization_barrier((x, ctx))
         ctx_own = lax.all_to_all(ctx.reshape(tp, chunk, width), 'tp', split_axis=0, concat_axis=0, tiled=True)
         x_rows = x_mlp.reshape(tokens, width)
-        rows = 512
-        nt = tokens // rows
+        rows, shards = 1024, 2
+        nt, nf = tokens // rows, tp // shards
         mlp = pl.pallas_call(
-            mlp_kernel,
-            grid=(tp, nt),
+            functools.partial(mlp_kernel, 256),
+            grid=(nf, nt),
             in_specs=[
                 pl.BlockSpec((rows, width), lambda f, t: (jnp.where(f == 0, t, nt - 1), 0)),
                 pl.BlockSpec((1, width), lambda f, t: (0, 0)),
                 pl.BlockSpec((1, width), lambda f, t: (0, 0)),
-                pl.BlockSpec((1, width, ff), lambda f, t: (f, 0, 0)),
-                pl.BlockSpec((1, ff, width), lambda f, t: (f, 0, 0)),
-            ],
-            out_specs=pl.BlockSpec((rows, width), lambda f, t: (jnp.where(f == tp - 1, t, 0), 0)),
+                pl.BlockSpec((shards, width, ff), lambda f, t: (f, 0, 0)),
+                pl.BlockSpec((shards, ff, width), lambda f, t: (f, 0, 0)),
+            ],
+            out_specs=pl.BlockSpec((rows, width), lambda f, t: (jnp.where(f == nf - 1, t, 0), 0)),
             out_shape=jax.ShapeDtypeStruct((tokens, width), F32),
             scratch_shapes=[pltpu.VMEM((tokens, width), BF16), pltpu.VMEM((tokens, width), F32)],
             compiler_params=params(('arbitrary', 'arbitrary')),
@@ -220,6 +246,8 @@
             name='mlp',
         )(x_rows, mlp_gain.reshape(1, width), mlp_bias.reshape(1, width), up_all, down_all)
 
+        rows = 512
+        nt = tokens // rows
         y = pl.pallas_call(
             final_kernel,
             grid=(nt,),

time: 316 us -> 263 us (0.83)
  Pallas kernels: 206 us -> 133 us
  waiting for transfers between devices: 2.41 us -> 23.1 us
    pallas_call x2, Pallas kernels: 169 us -> 99.8 us  [the longest x1 54.2 us: local_layer(): pl.pallas_call(functools.partial(attn_kernel, head_dim, q_rows, kv_cols),...]
    all_gather x1, waiting for transfers between devices: 0.02 us -> 20.8 us  [local_layer(): down_all = lax.all_gather(w_down, 'tp', axis=0, tiled=False)]
    pallas_call x1, Pallas kernels: 26 us -> 21.7 us  [local_layer(): pl.pallas_call(functools.partial(qkv_kernel, head_dim), grid=(tp // nb,),...]
  transfers between devices with their start and end apart: 5 -> 5, of which waited for: 1 -> 2; matrix products, arithmetic and copies ran while one was open for 2% -> 2% of each run, Pallas kernels for 62% -> 46%
where the time goes in v2:
time: 263 us; the launch traced here: 262 us
  Pallas kernels  133 us (51%)
  blocking collectives  80.2 us (30%)
  waiting for transfers between devices  23.1 us (9%)
  between operations  13.2 us (5%)
  other arithmetic  5.6 us (2%)
  starting transfers between devices  5 us (2%)
    all_to_all x1, blocking collectives, local_layer(): x_seq = lax.all_to_all(x, 'tp', split_axis=0, concat_axis=0, tiled=True)  80.2 us
    pallas_call x1, Pallas kernels, local_layer(): pl.pallas_call(functools.partial(attn_kernel, head_dim, q_rows, kv_cols),...  54.2 us
    pallas_call x1, Pallas kernels, local_layer(): pl.pallas_call(functools.partial(mlp_kernel, 256), grid=(nf, nt), in_spec...  45.6 us
    pallas_call x1, Pallas kernels, local_layer(): pl.pallas_call(functools.partial(qkv_kernel, head_dim), grid=(tp // nb,),...  21.7 us
    all_gather x1, waiting for transfers between devices, local_layer(): down_all = lax.all_gather(w_down, 'tp', axis=0, tiled=False)  20.8 us
    pallas_call x1, Pallas kernels, local_layer(): pl.pallas_call(final_kernel, grid=(nt,), in_specs=[pl.BlockSpec((rows, wi...  11.4 us
    mul x1, other arithmetic, local_layer(): cos_tab, sin_tab = (jnp.cos(angles), jnp.sin(angles) * sign[None, :])  5.58 us
  transfers between devices with their start and end apart: 5, of which 2 were waited for; matrix products, arithmetic and copies ran while one was open for 2% of the time, Pallas kernels for 46%

profile of v2, /device:TPU:81, one launch (start us, length us, event | category | flops | bytes accessed | tf_op | source)
XLA Modules:
  0.0 262.5 jit_solution(110703042497185294)
XLA Ops:
  6.5 0.0 all-gather.7.cloned.1.call-start
  6.6 1.2 copy.15
  7.7 1.2 copy.16
  8.9 0.1 all-gather.7.cloned.1.call-update
  9.0 0.0 copy-start
  9.0 0.1 all-gather.11.cloned.1.call-start
  9.0 80.2 %all_to_all.10.x_ref = bf16[8,256,1024]{2,1,0:T(8,128)(2,1)} all-to-all(bf16[8,256,1024]{2,1,0:T(8,128)(2,1)} %param.10), channel_id=1, replica_groups=mesh['dp'=4,'tp'=8] {'tp'}, dimensions={0} | all-to-all | bytes 8388608 | tf_op jit(solution)/shard_map/all_to_all | solution.py:168
  89.2 0.9 all-gather.7.cloned.1.call-done.w_ref
  90.2 0.1 all-gather.11.cloned.1.call-update
  90.3 0.1 all-gather.13.cloned.1.call-start
  90.3 0.7 all-gather.13.cloned.1.call-update
  91.0 0.0 copy-done
  91.1 0.1 mul.27
  91.2 5.6 %fusion = (f32[2048,128]{1,0:T(8,128)}, f32[2048,128]{1,0:T(8,128)}) fusion(f32[128]{0:T(128)S(1)} %compare_select_fusion, f32[128]{0:T(128)S(1)} %mul.27, f32[2048]{0:T(1024)S(1)} %convert_element_type.3), kind=kLoop, calls=%fused_computation.2 | loop fusion | flops 524288 | bytes 2106368 | tf_op jit(solution)/shard_map/mul | solution.py:175
  96.8 21.7 %qkv.1 = (bf16[8,2048,128]{2,1,0:T(8,128)(2,1)}, bf16[8,128,2048]{2,1,0:T(8,128)(2,1)}, bf16[8,2048,128]{2,1,0:T(8,128)(2,1)}) custom-call(bf16[8,256,1024]{2,1,0:T(8,128)(2,1)} %all_to_all.10.x_ref, bf16[8,1024,384]{2,1,0:T(8,128)(2,1)} %all-gather.7.cloned.1.call-done.w_ref, f32[2048,128]{1,0:T(8,128)} %get-tuple-element.22.cos_ref, ...), custom_call_target="tpu_custom_call" | custom-call | flops 12884901888 | bytes 23068672 | tf_op jit(solution)/shard_map/qkv/pallas_call | solution.py:179
  118.5 54.2 %attn.1 = bf16[2048,1024]{1,0:T(8,128)(2,1)} custom-call(bf16[8,2048,128]{2,1,0:T(8,128)(2,1)} %get-tuple-element.13.q_ref, bf16[8,128,2048]{2,1,0:T(8,128)(2,1)} %get-tuple-element.14.k_ref, bf16[8,2048,128]{2,1,0:T(8,128)(2,1)} %get-tuple-element.15.v_ref), custom_call_target="tpu_custom_call" | custom-call | flops 34359738368 | bytes 16777216 | tf_op jit(solution)/shard_map/attn/pallas_call | solution.py:206
  172.7 4.7 %all-to-all-start.1 = ((bf16[8,256,1024]{2,1,0:T(8,128)(2,1)}), bf16[8,256,1024]{2,1,0:T(8,128)(2,1)}, u32[]{:S(2)}, u32[]{:S(2)}) async-start(bf16[8,256,1024]{2,1,0:T(8,128)(2,1)} %bitcast.16), calls=%async_computation.1 | async-start | bytes 8388608 | tf_op jit(solution)/shard_map/all_to_all | solution.py:227
  177.5 0.1 all-gather.9.cloned.1.call-start
  177.6 0.5 all-gather.9.cloned.1.call-update
  178.1 0.0 all-gather.11.cloned.1.call-done
  178.1 20.8 %all-gather.13.cloned.1.call-done = bf16[4096,1024]{1,0:T(8,128)(2,1)} async-done(((bf16[512,1024]{1,0:T(8,128)(2,1)}), bf16[4096,1024]{1,0:T(8,128)(2,1)}) %all-gather.13.cloned.1.call-update) | async-done | bytes 8388624 | tf_op jit(solution)/shard_map/all_gather | solution.py:224
  198.9 45.6 %mlp.1.mlp_ref = f32[2048,1024]{1,0:T(8,128)} custom-call(bf16[2048,1024]{1,0:T(8,128)(2,1)} %bitcast.14, f32[1,1024]{1,0:T(1,128)} %bitcast.23, f32[1,1024]{1,0:T(1,128)} %bitcast.24, bf16[8,1024,512]{2,1,0:T(8,128)(2,1)} %bitcast.19, bf16[8,512,1024]{2,1,0:T(8,128)(2,1)} %bitcast.20), custom_call_target="tpu_custom_call" | custom-call | flops 34359738368 | bytes 16777216 | tf_op jit(solution)/shard_map/mlp/pallas_call | solution.py:231
  244.5 0.0 all-to-all-done.1
  244.5 0.0 all-gather.9.cloned.1.call-done.wo_ref
  244.5 11.4 %final.1 = bf16[2048,1024]{1,0:T(8,128)(2,1)} custom-call(bf16[2048,1024]{1,0:T(8,128)(2,1)} %bitcast.15, bf16[2048,1024]{1,0:T(8,128)(2,1)} %bitcast.7.ctx_ref, bf16[1024,1024]{1,0:T(8,128)(2,1)} %all-gather.9.cloned.1.call-done.wo_ref, f32[2048,1024]{1,0:T(8,128)} %mlp.1.mlp_ref), custom_call_target="tpu_custom_call" | custom-call | flops 4294967296 | bytes 20971520 | tf_op jit(solution)/shard_map/final/pallas_call | solution.py:251
  (4 shorter events, 0.0 us)
Async XLA Ops:
  6.5 83.6 %all-gather.7.cloned.1.call-start = ((), (), s32[]{:S(2)}) async-start(), calls=%async_computation.2 | async-start | bytes 7077888 | tf_op jit(solution)/shard_map/all_gather | solution.py:167
  9.0 82.1 %copy-start = (s32[2048]{0:T(1024)S(1)}, s32[2048]{0:T(1024)}, u32[]{:S(2)}) copy-start(s32[2048]{0:T(1024)} %param.19) | copy-start | bytes 24580
  9.0 169.1 %all-gather.11.cloned.1.call-start = ((), (), s32[]{:S(2)}) async-start(), calls=%async_computation.4 | async-start | bytes 9437184 | tf_op jit(solution)/shard_map/all_gather | solution.py:223
  90.3 108.7 %all-gather.13.cloned.1.call-start = ((), (), s32[]{:S(2)}) async-start(), calls=%async_computation.5 | async-start | bytes 9437184 | tf_op jit(solution)/shard_map/all_gather | solution.py:224
  172.7 71.8 %all-to-all-start.1 = ((bf16[8,256,1024]{2,1,0:T(8,128)(2,1)}), bf16[8,256,1024]{2,1,0:T(8,128)(2,1)}, u32[]{:S(2)}, u32[]{:S(2)}) async-start(bf16[8,256,1024]{2,1,0:T(8,128)(2,1)} %bitcast.16), calls=%async_computation.1 | async-start | bytes 8388608 | tf_op jit(solution)/shard_map/all_to_all | solution.py:227
  177.5 67.1 %all-gather.9.cloned.1.call-start = ((), (), s32[]{:S(2)}) async-start(), calls=%async_computation.3 | async-start | bytes 2359296 | tf_op jit(solution)/shard_map/all_gather | solution.py:225
Sparse Core Ops, SparseCore 0:
  9.1 81.0 all-gather.6
  91.8 48.0 all-gather.10
  141.5 57.3 all-gather.12
  200.4 29.3 all-gather.8

commit v3 on v2

--- a/solution.py
+++ b/solution.py
@@ -10,6 +10,7 @@
 BF16 = jnp.bfloat16
 F32 = jnp.float32
 VMEM_LIMIT = 60 * 1024 * 1024
+MESH = pl.DeviceIdType.MESH
 
 
 def norm_rows(rows, gain, bias):
@@ -48,8 +49,40 @@
         v_ref[p + 1] = vals[:, pair:]
 
 
-def attn_kernel(head_dim, rows, chunk, q_ref, k_ref, v_ref, o_ref, s_ref):
-    seq, pair = o_ref.shape
+def attn_kernel(head_dim, rows, chunk, q_ref, k_ref, v_ref, ctx_ref, s_ref, o_ref, send, recv, own_sem):
+    p, me, tp = pl.program_id(0), lax.axis_index('tp'), ctx_ref.shape[0]
+    seq, pair = o_ref.shape[1:]
+    tok = seq // tp
+    slot = lax.rem(p, 2)
+
+    def ship(step, r):
+        to, lane_cols = lax.rem(me + r, tp), pl.ds(pl.multiple_of(step * pair, pair), pair)
+        src = o_ref.at[lax.rem(step, 2), pl.ds(pl.multiple_of(to * tok, tok), tok), :]
+        return pltpu.make_async_remote_copy(
+            src_ref=src, dst_ref=ctx_ref.at[me, :, lane_cols], send_sem=send.at[lax.rem(step, 2), r], recv_sem=recv.at[step, r],
+            device_id={'tp': to}, device_id_type=MESH)
+
+    def keep(step):
+        lane_cols = pl.ds(pl.multiple_of(step * pair, pair), pair)
+        src = o_ref.at[lax.rem(step, 2), pl.ds(pl.multiple_of(me * tok, tok), tok), :]
+        return pltpu.make_async_copy(src, ctx_ref.at[me, :, lane_cols], own_sem.at[lax.rem(step, 2)])
+
+    def drain(step):
+        for r in range(1, tp):
+            ship(step, r).wait_send()
+        keep(step).wait()
+
+    @pl.when(p == 0)
+    def _():
+        barrier = pltpu.get_barrier_semaphore()
+        for r in range(1, tp):
+            pl.semaphore_signal(barrier, inc=1, device_id={'tp': lax.rem(me + r, tp)}, device_id_type=MESH)
+        pl.semaphore_wait(barrier, tp - 1)
+
+    @pl.when(p >= 2)
+    def _():
+        drain(p - 2)
+
     units = [(r, h) for r in range(0, seq, rows) for h in range(pair // head_dim)]
     lane = lax.broadcasted_iota(jnp.int32, (rows, pair), 1)
 
@@ -102,41 +135,197 @@
                 total, acc = weigh(n % 2, m, starts(unit)[j], total, acc)
         r, h = unit
         out = (acc / jnp.sum(total, axis=1, keepdims=True)).astype(BF16)
-        o_ref[r:r + rows, h * head_dim:(h + 1) * head_dim] = out[:, h * head_dim:(h + 1) * head_dim]
-
-
-def mlp_kernel(sub, x_ref, gain_ref, bias_ref, up_ref, down_ref, o_ref, m_ref, acc_ref):
-    f, t = pl.program_id(0), pl.program_id(1)
-    rows, width = x_ref.shape
-    shards, ff = up_ref.shape[0], up_ref.shape[2]
-    base = pl.multiple_of(t * rows, rows)
-
-    @pl.when(f == 0)
+        o_ref[slot, r:r + rows, h * head_dim:(h + 1) * head_dim] = out[:, h * head_dim:(h + 1) * head_dim]
+
+    for r in range(1, tp):
+        ship(p, r).start()
+    keep(p).start()
+
+    @pl.when(p == pl.num_programs(0) - 1)
     def _():
-        for h in range(0, rows, sub):
-            part = pl.ds(base + h, sub)
-            m_ref[part, :] = norm_rows(x_ref[h:h + sub, :], gain_ref[...], bias_ref[...])
-            acc_ref[part, :] = jnp.zeros((sub, width), F32)
-
-    down_w = down_ref[...].reshape(shards * ff, width)
-
-    def expand(h):
-        rows_in = m_ref[pl.ds(base + h, sub), :]
-        return [jnp.dot(rows_in, up_ref[k], preferred_element_type=F32) for k in range(shards)]
+        drain(p - 1)
+        drain(p)
+        for step in range(recv.shape[0]):
+            for r in range(1, tp):
+                ship(step, r).wait_recv()
+
+
+def exchange_kernel(sub, x_ref, gain_ref, bias_ref, up_ref, down_ref, wqkv_ref, wo_ref,
+                    xs_ref, wqkv_all, wo_all, acc_ref, up_all, down_all, m_ref, send, recv, xsend, xrecv, own_sem):
+    me, tp = lax.axis_index('tp'), xs_ref.shape[0]
+    dp = lax.axis_index('dp')
+    hz = lax.rem(dp, 2)
+    twin = dp + 1 - 2 * hz
+    core = lax.rem(me, 2)
+    sib = me + 1 - 2 * core
+    right, left, far = lax.rem(me + 2, tp), lax.rem(me + tp - 2, tp), lax.rem(me + 4, tp)
+    tokens, width = acc_ref.shape
+
+    barrier = pltpu.get_barrier_semaphore()
+    for r in range(1, tp):
+        pl.semaphore_signal(barrier, inc=1, device_id={'tp': lax.rem(me + r, tp)}, device_id_type=MESH)
+    pl.semaphore_signal(barrier, inc=1, device_id={'dp': twin}, device_id_type=MESH)
+    pl.semaphore_wait(barrier, tp)
+
+    weights = ((up_ref, up_all, True), (down_ref, down_all, True), (wqkv_ref, wqkv_all, False), (wo_ref, wo_all, True))
+    UP, DOWN, QKV, OUT = range(4)
+
+    def whole(ref, shared):
+        return ref.at[hz] if shared else ref
+
+    def link(w, k):
+        own, every, shared = weights[w]
+        rows = own.shape[1]
+
+        def part(s):
+            return whole(every.at[s], shared)
+
+        def quarter(s, n):
+            if shared:
+                return every.at[s, hz, n * (rows // 2):(n + 1) * (rows // 2), :]
+            return every.at[s, n]
+
+        if k == 0:
+            src, dst, dev = whole(own, shared), part(me), {'tp': right}
+        elif k == 1:
+            src, dst, dev = whole(own, shared), part(me), {'tp': left}
+        elif k == 2:
+            src, dst, dev = own, every.at[me], {'tp': sib}
+        elif k == 3:
+            src, dst, dev = quarter(left, 0), quarter(left, 0), {'tp': right}
+        elif k == 4:
+            src, dst, dev = quarter(right, 1), quarter(right, 1), {'tp': left}
+        elif k < 8:
+            s = (left, right, far)[k - 5]
+            src, dst, dev = part(s), part(s), {'dp': twin}
+        elif k < 11:
+            s = (left, right, far)[k - 8]
+            src, dst, dev = part(s), part(s), {'tp': sib}
+        else:
+            s = (left, right, far)[k - 11]
+            src, dst, dev = every.at[s, 1 - hz], every.at[s, 1 - hz], {'tp': sib}
+        return pltpu.make_async_remote_copy(src_ref=src, dst_ref=dst, send_sem=send.at[w, k], recv_sem=recv.at[w, k], device_id=dev, device_id_type=MESH)
+
+    started = []
+
+    def go(w, *kinds):
+        for k in kinds:
+            link(w, k).start()
+            started.append((w, k))
+
+    def arrived(w, *kinds):
+        for k in kinds:
+            link(w, k).wait_recv()
+
+    def near(w):
+        shared = weights[w][2]
+        arrived(w, 0, 1)
+        go(w, 3, 4)
+        if shared:
+            go(w, 5, 6)
+        go(w, 8, 9)
+
+    def distant(w):
+        shared = weights[w][2]
+        arrived(w, 3, 4)
+        if shared:
+            go(w, 7)
+        go(w, 10)
+
+    def token_block(r):
+        to = lax.rem(me + r, tp)
+        return pltpu.make_async_remote_copy(src_ref=x_ref.at[to], dst_ref=xs_ref.at[me], send_sem=xsend.at[r], recv_sem=xrecv.at[r], device_id={'tp': to}, device_id_type=MESH)
 
     def gelu(pre):
         return (0.5 * pre * (1.0 + lax.erf(pre * (0.5 ** 0.5)))).astype(BF16)
 
-    pre = expand(0)
-    for h in range(0, rows, sub):
-        following = expand(h + sub) if h + sub < rows else None
-        act = jnp.concatenate([gelu(p) for p in pre], axis=1)
-        acc_ref[pl.ds(base + h, sub), :] += jnp.dot(act, down_w, preferred_element_type=F32)
-        pre = following
-
-    @pl.when(f == pl.num_programs(0) - 1)
-    def _():
-        o_ref[...] = acc_ref[pl.ds(base, rows), :]
+    def mlp(first, parts):
+        ups = [p[0] for p in parts]
+        downs = [p[1] for p in parts]
+
+        def body(t, carry):
+            base = pl.multiple_of(t * 2 * sub, 2 * sub)
+
+            def expand(h):
+                rows_in = m_ref[pl.ds(base + h * sub, sub), :]
+                return [jnp.dot(rows_in, u[...], preferred_element_type=F32) for u in ups]
+
+            pre = expand(0)
+            for h in range(2):
+                following = expand(1) if h == 0 else None
+                act = jnp.concatenate([gelu(p) for p in pre], axis=1)
+                down_w = jnp.concatenate([d[...] for d in downs], axis=0)
+                out = jnp.dot(act, down_w, preferred_element_type=F32)
+                rows_out = pl.ds(base + h * sub, sub)
+                if first:
+                    acc_ref[rows_out, :] = out
+                else:
+                    acc_ref[rows_out, :] += out
+                pre = following
+            return carry
+
+        lax.fori_loop(0, tokens // (2 * sub), body, 0)
+
+    def halves(s, n):
+        return up_all.at[s, n], down_all.at[s, n]
+
+    local = [
+        pltpu.make_async_copy(wqkv_ref, wqkv_all.at[me], own_sem.at[0]),
+        pltpu.make_async_copy(wo_ref, wo_all.at[me], own_sem.at[1]),
+        pltpu.make_async_copy(x_ref.at[me], xs_ref.at[me], own_sem.at[2]),
+    ]
+    for w in (UP, DOWN, QKV, OUT):
+        go(w, 0, 1, 2)
+    for copy in local:
+        copy.start()
+
+    def norm(t, carry):
+        tok = x_ref.shape[1]
+        m_ref[pl.ds(pl.multiple_of(t * tok, tok), tok), :] = norm_rows(x_ref[t], gain_ref[...], bias_ref[...])
+        return carry
+
+    lax.fori_loop(0, tp, norm, 0)
+    arrived(UP, 2)
+    arrived(DOWN, 2)
+    near(UP)
+    mlp(True, [(up_ref.at[0], down_ref.at[0]), (up_ref.at[1], down_ref.at[1]), halves(sib, 0), halves(sib, 1)])
+    near(DOWN)
+    distant(UP)
+    near(OUT)
+    arrived(UP, 8, 9)
+    arrived(DOWN, 8, 9)
+    sib_left, sib_right, sib_far = left + 1 - 2 * core, right + 1 - 2 * core, far + 1 - 2 * core
+    near(QKV)
+    for r in range(1, tp):
+        token_block(r).start()
+    mlp(False, [halves(left, hz), halves(right, hz), halves(sib_left, hz), halves(sib_right, hz)])
+    distant(DOWN)
+    distant(OUT)
+    distant(QKV)
+    for w in (UP, DOWN):
+        arrived(w, 5, 6)
+        go(w, 11, 12)
+    arrived(UP, 11, 12)
+    arrived(DOWN, 11, 12)
+    mlp(False, [halves(left, 1 - hz), halves(right, 1 - hz), halves(sib_left, 1 - hz), halves(sib_right, 1 - hz)])
+    for w in (UP, DOWN):
+        arrived(w, 7)
+        go(w, 13)
+    for w in (UP, DOWN):
+        arrived(w, 10, 13)
+    mlp(False, [halves(far, hz), halves(far, 1 - hz), halves(sib_far, hz), halves(sib_far, 1 - hz)])
+    arrived(OUT, 5, 6, 7)
+    go(OUT, 11, 12, 13)
+    arrived(QKV, 2, 8, 9, 10)
+    arrived(OUT, 2, 8, 9, 10, 11, 12, 13)
+    for r in range(1, tp):
+        token_block(r).wait_recv()
+    for w, k in started:
+        link(w, k).wait_send()
+    for r in range(1, tp):
+        token_block(r).wait_send()
+    for copy in local:
+        copy.wait()
 
 
 def final_kernel(x_ref, ctx_ref, wo_ref, mlp_ref, y_ref):
@@ -164,9 +353,37 @@
         half = head_dim // 2
 
         w_qkv = w_qkv.reshape(width, groups, 3, head_dim).swapaxes(1, 2).reshape(width, 3 * pair)
-        wqkv_all = lax.all_gather(w_qkv, 'tp', axis=0, tiled=False)
-        x_seq = lax.all_to_all(x, 'tp', split_axis=0, concat_axis=0, tiled=True)
-        x_seq = x_seq.reshape(tp, chunk, width)
+        half_ff = ff // 2
+        vmem = pl.BlockSpec(memory_space=pltpu.VMEM)
+        hbm = pl.BlockSpec(memory_space=pl.ANY)
+        x_seq, wqkv_all, wo_all, mlp = pl.pallas_call(
+            functools.partial(exchange_kernel, 256),
+            in_specs=[vmem] * 7,
+            out_specs=[hbm, hbm, hbm, vmem],
+            out_shape=[
+                jax.ShapeDtypeStruct((tp, chunk, width), BF16),
+                jax.ShapeDtypeStruct((tp, 2, width // 2, 3 * pair), BF16),
+                jax.ShapeDtypeStruct((tp, 2, ctx_cols // 2, width), BF16),
+                jax.ShapeDtypeStruct((tokens, width), F32),
+            ],
+            scratch_shapes=[
+                pltpu.VMEM((tp, 2, width, half_ff), BF16),
+                pltpu.VMEM((tp, 2, half_ff, width), BF16),
+                pltpu.VMEM((tokens, width), BF16),
+                pltpu.SemaphoreType.DMA((4, 14)),
+                pltpu.SemaphoreType.DMA((4, 14)),
+                pltpu.SemaphoreType.DMA((tp,)),
+                pltpu.SemaphoreType.DMA((tp,)),
+                pltpu.SemaphoreType.DMA((3,)),
+            ],
+            compiler_params=pltpu.CompilerParams(vmem_limit_bytes=VMEM_LIMIT, collective_id=0, has_side_effects=True),
+            cost_estimate=pl.CostEstimate(flops=4 * tokens * width * ff * tp, bytes_accessed=4 * tokens * width * 2, transcendentals=0),
+            name='exchange',
+        )(x, mlp_gain.reshape(1, width), mlp_bias.reshape(1, width),
+          w_up.reshape(width, 2, half_ff).swapaxes(0, 1), w_down.reshape(2, half_ff, width),
+          w_qkv.reshape(2, width // 2, 3 * pair), w_out.reshape(2, ctx_cols // 2, width))
+        wqkv_all = wqkv_all.reshape(tp, width, 3 * pair)
+        wo_all = wo_all.reshape(tp * ctx_cols, width)
 
         inv_freq = 10000.0 ** (-2.0 * jnp.arange(half, dtype=F32) / head_dim)
         inv_freq = jnp.tile(inv_freq, 2 * groups)
@@ -211,41 +428,21 @@
                 pl.BlockSpec((1, pair, seq), lambda p: (p, 0, 0)),
                 pl.BlockSpec((1, seq, pair), lambda p: (p, 0, 0)),
             ],
-            out_specs=pl.BlockSpec((seq, pair), lambda p: (0, p)),
-            out_shape=jax.ShapeDtypeStruct((seq, tp * pair), BF16),
-            scratch_shapes=[pltpu.VMEM((2, q_rows, seq), F32)],
-            compiler_params=params(('arbitrary',)),
+            out_specs=hbm,
+            out_shape=jax.ShapeDtypeStruct((tp, chunk, tp * pair), BF16),
+            scratch_shapes=[
+                pltpu.VMEM((2, q_rows, seq), F32),
+                pltpu.VMEM((2, seq, pair), BF16),
+                pltpu.SemaphoreType.DMA((2, tp)),
+                pltpu.SemaphoreType.DMA((tp, tp)),
+                pltpu.SemaphoreType.DMA((2,)),
+            ],
+            compiler_params=pltpu.CompilerParams(dimension_semantics=('arbitrary',), vmem_limit_bytes=VMEM_LIMIT, collective_id=1, has_side_effects=True),
             cost_estimate=pl.CostEstimate(flops=8 * seq * seq * pair * tp, bytes_accessed=2 * seq * width * 4, transcendentals=0),
             name='attn',
         )(q, k, v)
 
-        w_up, w_down, w_out, _, _ = lax.optimization_barrier((w_up, w_down, w_out, wqkv_all, x_seq))
-        up_all = lax.all_gather(w_up, 'tp', axis=0, tiled=False)
-        down_all = lax.all_gather(w_down, 'tp', axis=0, tiled=False)
-        wo_all = lax.all_gather(w_out, 'tp', axis=0, tiled=True)
-        x_mlp, ctx = lax.optimization_barrier((x, ctx))
-        ctx_own = lax.all_to_all(ctx.reshape(tp, chunk, width), 'tp', split_axis=0, concat_axis=0, tiled=True)
-        x_rows = x_mlp.reshape(tokens, width)
-        rows, shards = 1024, 2
-        nt, nf = tokens // rows, tp // shards
-        mlp = pl.pallas_call(
-            functools.partial(mlp_kernel, 256),
-            grid=(nf, nt),
-            in_specs=[
-                pl.BlockSpec((rows, width), lambda f, t: (jnp.where(f == 0, t, nt - 1), 0)),
-                pl.BlockSpec((1, width), lambda f, t: (0, 0)),
-                pl.BlockSpec((1, width), lambda f, t: (0, 0)),
-                pl.BlockSpec((shards, width, ff), lambda f, t: (f, 0, 0)),
-                pl.BlockSpec((shards, ff, width), lambda f, t: (f, 0, 0)),
-            ],
-            out_specs=pl.BlockSpec((rows, width), lambda f, t: (jnp.where(f == nf - 1, t, 0), 0)),
-            out_shape=jax.ShapeDtypeStruct((tokens, width), F32),
-            scratch_shapes=[pltpu.VMEM((tokens, width), BF16), pltpu.VMEM((tokens, width), F32)],
-            compiler_params=params(('arbitrary', 'arbitrary')),
-            cost_estimate=pl.CostEstimate(flops=4 * tokens * width * ff * tp, bytes_accessed=4 * tokens * width * 2, transcendentals=0),
-            name='mlp',
-        )(x_rows, mlp_gain.reshape(1, width), mlp_bias.reshape(1, width), up_all, down_all)
-
+        x_rows = x.reshape(tokens, width)
         rows = 512
         nt = tokens // rows
         y = pl.pallas_call(
@@ -262,7 +459,7 @@
             compiler_params=params(('arbitrary',)),
             cost_estimate=pl.CostEstimate(flops=2 * tokens * width * width, bytes_accessed=tokens * width * 10, transcendentals=0),
             name='final',
-        )(x_rows, ctx_own.reshape(tokens, width), wo_all, mlp)
+        )(x_rows, ctx.reshape(tokens, width), wo_all, mlp)
         return y.reshape(batch, chunk, width)
 
     return jax.shard_map(local_layer, mesh=mesh, in_specs=(P('dp', 'tp', None), P(), P(), P(), P(), P(None, 'tp', None), P('tp', None), P(None, 'tp'), P('tp', None), P()), out_specs=P('dp', 'tp', None), check_vma=False)

time: 263 us -> 239 us (0.909)
  Pallas kernels: 133 us -> 227 us
  blocking collectives: 80.2 us -> 0 us
  waiting for transfers between devices: 23.1 us -> 0 us
  between operations: 13.2 us -> 0.05 us
  starting transfers between devices: 5 us -> 0 us
  local copies, waits for them, and re-layouts: 2.43 us -> 5.55 us
    all_to_all x1 -> x0, blocking collectives: 80.2 us -> none  [local_layer(): x_seq = lax.all_to_all(x, 'tp', split_axis=0, concat_axis=0, tiled=True)]
    pallas_call x1, Pallas kernels: 45.6 us -> 123 us  [local_layer(): pl.pallas_call(functools.partial(exchange_kernel, 256), in_specs=[vmem] *...]
    all_gather x4 -> x0, waiting for transfers between devices: 21.8 us -> none  [the longest x1 20.8 us: local_layer(): down_all = lax.all_gather(w_down, 'tp', axis=0, tiled=False)]
    pallas_call x1, Pallas kernels: 54.2 us -> 70.5 us  [local_layer(): pl.pallas_call(functools.partial(attn_kernel, head_dim, q_rows, kv_cols),...]
    all_to_all x1 -> x0, starting transfers between devices: 4.74 us -> none  [local_layer(): lax.all_to_all(ctx.reshape(tp, chunk, width), 'tp', split_axis=0, concat_...]
  transfers between devices with their start and end apart: 5 -> 0, of which waited for: 2 -> 0; matrix products, arithmetic and copies ran while one was open for 2% -> 0% of each run, Pallas kernels for 46% -> 0%
where the time goes in v3:
time: 239 us
  Pallas kernels  227 us (95%)
  other arithmetic  6.37 us (3%)
  local copies, waits for them, and re-layouts  5.55 us (2%)
    pallas_call x1, Pallas kernels, local_layer(): pl.pallas_call(functools.partial(exchange_kernel, 256), in_specs=[vmem] *...  123 us
    pallas_call x1, Pallas kernels, local_layer(): pl.pallas_call(functools.partial(attn_kernel, head_dim, q_rows, kv_cols),...  70.5 us
    pallas_call x1, Pallas kernels, local_layer(): pl.pallas_call(functools.partial(qkv_kernel, head_dim), grid=(tp // nb,),...  22 us
    pallas_call x1, Pallas kernels, local_layer(): pl.pallas_call(final_kernel, grid=(nt,), in_specs=[pl.BlockSpec((rows, wi...  11.4 us
    mul x1, other arithmetic, local_layer(): cos_tab, sin_tab = (jnp.cos(angles), jnp.sin(angles) * sign[None, :])  5.59 us

profile of v3, /device:TPU:81, one launch (start us, length us, event | category | flops | bytes accessed | tf_op | source)
XLA Modules:
  0.0 239.0 jit_solution(7173982081295363836)
XLA Ops:
  0.0 0.0 copy-start
  0.0 0.1 mul.27
  0.1 0.8 convert_element_type.3
  0.9 1.2 copy.17
  2.1 0.6 reshape_reshape.3
  2.6 1.9 copy.15.wqkv_ref
  4.5 0.0 copy-done
  4.5 0.5 copy.12
  5.1 1.3 copy.13
  6.4 5.6 %fusion = (f32[2048,128]{1,0:T(8,128)}, f32[2048,128]{1,0:T(8,128)}) fusion(f32[128]{0:T(128)S(1)} %compare_select_fusion, f32[128]{0:T(128)S(1)} %mul.27, f32[2048]{0:T(1024)S(1)} %convert_element_type.3), kind=kLoop, calls=%fused_computation.2 | loop fusion | flops 524288 | bytes 2106368 | tf_op jit(solution)/shard_map/mul | solution.py:392
  12.0 123.2 %exchange.1 = (bf16[8,256,1024]{2,1,0:T(8,128)(2,1)}, bf16[8,2,512,384]{3,2,1,0:T(8,128)(2,1)}, bf16[8,2,64,1024]{3,2,1,0:T(8,128)(2,1)}, f32[2048,1024]{1,0:T(8,128)}) custom-call(bf16[8,256,1024]{2,1,0:T(8,128)(2,1)} %x_ref.1, f32[1,1024]{1,0:T(1,128)} %bitcast.30, f32[1,1024]{1,0:T(1,128)} %bitcast.31, bf16[2,1024,256]{2,1,0:T(8,128)(2,1)} %bitcast.26, ...), custom_call_target="tpu_custom_call" | custom-call | flops 34359738368 | bytes 16777216 | tf_op jit(solution)/shard_map/exchange/pallas_call | solution.py:359
  135.2 22.0 %qkv.1 = (bf16[8,2048,128]{2,1,0:T(8,128)(2,1)}, bf16[8,128,2048]{2,1,0:T(8,128)(2,1)}, bf16[8,2048,128]{2,1,0:T(8,128)(2,1)}) custom-call(bf16[8,256,1024]{2,1,0:T(8,128)(2,1)} %get-tuple-element.12.x_ref, bf16[8,1024,384]{2,1,0:T(8,128)(2,1)} %bitcast.34, f32[2048,128]{1,0:T(8,128)} %get-tuple-element.20.cos_ref, f32[2048,128]{1,0:T(8,128)} %get-tuple-element.19.sin_ref, ...), custom_call_target="tpu_custom_call" | custom-call | flops 12884901888 | bytes 23068672 | tf_op jit(solution)/shard_map/qkv/pallas_call | solution.py:396
  157.1 70.5 %attn.1 = bf16[8,256,1024]{2,1,0:T(8,128)(2,1)} custom-call(bf16[8,2048,128]{2,1,0:T(8,128)(2,1)} %get-tuple-element.14.q_ref, bf16[8,128,2048]{2,1,0:T(8,128)(2,1)} %get-tuple-element.15.k_ref, bf16[8,2048,128]{2,1,0:T(8,128)(2,1)} %get-tuple-element.16.v_ref), custom_call_target="tpu_custom_call" | custom-call | flops 34359738368 | bytes 16777216 | tf_op jit(solution)/shard_map/attn/pallas_call | solution.py:423
  227.7 11.4 %final.1 = bf16[2048,1024]{1,0:T(8,128)(2,1)} custom-call(bf16[2048,1024]{1,0:T(8,128)(2,1)} %bitcast.22, bf16[2048,1024]{1,0:T(8,128)(2,1)} %bitcast.23, bf16[1024,1024]{1,0:T(8,128)(2,1)} %bitcast.25, f32[2048,1024]{1,0:T(8,128)} %get-tuple-element.18.mlp_ref), custom_call_target="tpu_custom_call" | custom-call | flops 4294967296 | bytes 20971520 | tf_op jit(solution)/shard_map/final/pallas_call | solution.py:448
  (3 shorter events, 0.0 us)
Async XLA Ops:
  0.0 4.5 %copy-start = (bf16[1024,512]{1,0:T(8,128)(2,1)S(1)}, bf16[1024,512]{1,0:T(8,128)(2,1)}, u32[]{:S(2)}) copy-start(bf16[1024,512]{1,0:T(8,128)(2,1)} %param.17) | copy-start | bytes 3145732

commit v4 on v3

--- a/solution.py
+++ b/solution.py
@@ -13,6 +13,37 @@
 MESH = pl.DeviceIdType.MESH
 
 
+OUTWARD, FORWARD = (0, 1), (7, 8)
+SEAT = (0, 8, 1, 4, 2, 5, 3, 6, 7)
+DIRECT, LANDING = (0, 1, 2, 3, 4, 5, 6), (2, 3, 4, 5, 6, 7, 8)
+
+
+class Places:
+    def __init__(self, tp):
+        self.me = lax.axis_index('tp')
+        self.core = lax.rem(self.me, 2)
+        self.right, self.left, self.far = lax.rem(self.me + 2, tp), lax.rem(self.me + tp - 2, tp), lax.rem(self.me + 4, tp)
+        self.sib = self.other(self.me)
+        self.left_sib, self.right_sib, self.far_sib = self.other(self.left), self.other(self.right), self.other(self.far)
+
+    def other(self, device):
+        return device + 1 - 2 * self.core
+
+    def route(self, kind):
+        me, left, right = self.me, self.left, self.right
+        return (
+            (right, self.far, None, 0),
+            (left, self.far_sib, None, 1),
+            (self.sib, self.sib, me, None),
+            (right, right, me, None),
+            (left, left, me, None),
+            (self.right_sib, self.right_sib, me, None),
+            (self.left_sib, self.left_sib, me, None),
+            (right, None, left, None),
+            (self.left_sib, None, right, None),
+        )[kind]
+
+
 def norm_rows(rows, gain, bias):
     rows32 = rows.astype(F32)
     mean = jnp.mean(rows32, axis=-1, keepdims=True)
@@ -26,41 +57,23 @@
     return jnp.where(lane_mod < half, pltpu.roll(vals, width - half, 1), pltpu.roll(vals, half, 1))
 
 
-def qkv_kernel(head_dim, x_ref, w_ref, cos_ref, sin_ref, gain_ref, bias_ref, q_ref, k_ref, v_ref):
-    blocks, rows, width = x_ref.shape
-    normed = norm_rows(x_ref[...].reshape(blocks * rows, width), gain_ref[...], bias_ref[...])
-    pair = q_ref.shape[2]
-    cos_tab, sin_tab = cos_ref[...], sin_ref[...]
-    lane_mod = lax.broadcasted_iota(jnp.int32, cos_tab.shape, 1) % head_dim
-    scale = head_dim ** -0.5
-
-    def rotate(vals):
-        vals = vals.astype(BF16).astype(F32)
-        return (vals * cos_tab + swap_halves(vals, lane_mod, head_dim // 2) * sin_tab).astype(BF16)
-
-    for p in range(0, w_ref.shape[0], 2):
-        for h in range(2):
-            qk = jnp.dot(normed, w_ref[p + h, :, :2 * pair], preferred_element_type=F32)
-            q_ref[p + h] = (rotate(qk[:, :pair]).astype(F32) * scale).astype(BF16)
-            k_ref[p + h] = rotate(qk[:, pair:]).astype(F32).T.astype(BF16)
-        w_val = jnp.concatenate([w_ref[p, :, 2 * pair:], w_ref[p + 1, :, 2 * pair:]], axis=1)
-        vals = jnp.dot(normed, w_val, preferred_element_type=F32).astype(BF16)
-        v_ref[p] = vals[:, :pair]
-        v_ref[p + 1] = vals[:, pair:]
-
-
-def attn_kernel(head_dim, rows, chunk, q_ref, k_ref, v_ref, ctx_ref, s_ref, o_ref, send, recv, own_sem):
-    p, me, tp = pl.program_id(0), lax.axis_index('tp'), ctx_ref.shape[0]
+def attn_kernel(head_dim, rows, chunk, q_ref, k_ref, v_ref, ctx_ref, s_ref, o_ref, relay_ref, send, recv, own_sem):
+    p, tp = pl.program_id(0), ctx_ref.shape[0]
+    place = Places(tp)
+    me = place.me
     seq, pair = o_ref.shape[1:]
     tok = seq // tp
     slot = lax.rem(p, 2)
 
-    def ship(step, r):
-        to, lane_cols = lax.rem(me + r, tp), pl.ds(pl.multiple_of(step * pair, pair), pair)
-        src = o_ref.at[lax.rem(step, 2), pl.ds(pl.multiple_of(to * tok, tok), tok), :]
-        return pltpu.make_async_remote_copy(
-            src_ref=src, dst_ref=ctx_ref.at[me, :, lane_cols], send_sem=send.at[lax.rem(step, 2), r], recv_sem=recv.at[step, r],
-            device_id={'tp': to}, device_id_type=MESH)
+    def ship(step, kind):
+        to, block, origin, relay = place.route(kind)
+        lane_cols = pl.ds(pl.multiple_of(step * pair, pair), pair)
+        if kind in FORWARD:
+            src = relay_ref.at[step, FORWARD.index(kind)]
+        else:
+            src = o_ref.at[lax.rem(step, 2), pl.ds(pl.multiple_of(block * tok, tok), tok), :]
+        dst = ctx_ref.at[origin, :, lane_cols] if relay is None else relay_ref.at[step, relay]
+        return pltpu.make_async_remote_copy(src_ref=src, dst_ref=dst, send_sem=send.at[step, kind], recv_sem=recv.at[step, kind], device_id={'tp': to}, device_id_type=MESH)
 
     def keep(step):
         lane_cols = pl.ds(pl.multiple_of(step * pair, pair), pair)
@@ -68,9 +81,14 @@
         return pltpu.make_async_copy(src, ctx_ref.at[me, :, lane_cols], own_sem.at[lax.rem(step, 2)])
 
     def drain(step):
-        for r in range(1, tp):
-            ship(step, r).wait_send()
+        for kind in DIRECT:
+            ship(step, kind).wait_send()
         keep(step).wait()
+
+    def pass_on(step):
+        for out, kind in zip(OUTWARD, FORWARD):
+            ship(step, out).wait_recv()
+            ship(step, kind).start()
 
     @pl.when(p == 0)
     def _():
@@ -137,28 +155,39 @@
         out = (acc / jnp.sum(total, axis=1, keepdims=True)).astype(BF16)
         o_ref[slot, r:r + rows, h * head_dim:(h + 1) * head_dim] = out[:, h * head_dim:(h + 1) * head_dim]
 
-    for r in range(1, tp):
-        ship(p, r).start()
+    for kind in DIRECT:
+        ship(p, kind).start()
     keep(p).start()
+
+    @pl.when(p >= 1)
+    def _():
+        pass_on(p - 1)
 
     @pl.when(p == pl.num_programs(0) - 1)
     def _():
+        pass_on(p)
         drain(p - 1)
         drain(p)
         for step in range(recv.shape[0]):
-            for r in range(1, tp):
-                ship(step, r).wait_recv()
-
-
-def exchange_kernel(sub, x_ref, gain_ref, bias_ref, up_ref, down_ref, wqkv_ref, wo_ref,
-                    xs_ref, wqkv_all, wo_all, acc_ref, up_all, down_all, m_ref, send, recv, xsend, xrecv, own_sem):
-    me, tp = lax.axis_index('tp'), xs_ref.shape[0]
+            for kind in FORWARD:
+                ship(step, kind).wait_send()
+            for kind in LANDING:
+                ship(step, kind).wait_recv()
+
+
+def exchange_kernel(sub, head_dim, x_ref, mgain_ref, mbias_ref, again_ref, abias_ref, up_ref, down_ref, wqkv_ref, wo_ref, cos4_ref, sin4_ref,
+                    q_ref, k_ref, v_ref, wo_all, mlp_ref,
+                    xs_ref, wqkv_all, up_all, down_all, m_ref, acc_ref, relay_ref, cos_ref, sin_ref, q_st, k_st, v_st,
+                    send, recv, xsend, xrecv, own_sem, out_sem):
+    tp = xs_ref.shape[0]
+    place = Places(tp)
+    me, core, sib = place.me, place.core, place.sib
+    right, left, far = place.right, place.left, place.far
     dp = lax.axis_index('dp')
     hz = lax.rem(dp, 2)
     twin = dp + 1 - 2 * hz
-    core = lax.rem(me, 2)
-    sib = me + 1 - 2 * core
-    right, left, far = lax.rem(me + 2, tp), lax.rem(me + tp - 2, tp), lax.rem(me + 4, tp)
+    tok = x_ref.shape[1]
+    pair = q_ref.shape[2]
     tokens, width = acc_ref.shape
 
     barrier = pltpu.get_barrier_semaphore()
@@ -170,12 +199,19 @@
     weights = ((up_ref, up_all, True), (down_ref, down_all, True), (wqkv_ref, wqkv_all, False), (wo_ref, wo_all, True))
     UP, DOWN, QKV, OUT = range(4)
 
+    half_ff = up_all.shape[3]
+
+    def up_cols(n):
+        start = n * half_ff
+        return up_ref.at[:, pl.ds(start if isinstance(n, int) else pl.multiple_of(start, half_ff), half_ff)]
+
     def whole(ref, shared):
         return ref.at[hz] if shared else ref
 
     def link(w, k):
         own, every, shared = weights[w]
-        rows = own.shape[1]
+        rows = every.shape[2]
+        mine = up_cols(hz) if w == UP else whole(own, shared)
 
         def part(s):
             return whole(every.at[s], shared)
@@ -186,11 +222,13 @@
             return every.at[s, n]
 
         if k == 0:
-            src, dst, dev = whole(own, shared), part(me), {'tp': right}
+            src, dst, dev = mine, part(me), {'tp': right}
         elif k == 1:
-            src, dst, dev = whole(own, shared), part(me), {'tp': left}
+            src, dst, dev = mine, part(me), {'tp': left}
         elif k == 2:
-            src, dst, dev = own, every.at[me], {'tp': sib}
+            src, dst, dev = (up_cols(0), every.at[me, 0], {'tp': sib}) if w == UP else (own, every.at[me], {'tp': sib})
+        elif k == 14:
+            src, dst, dev = up_cols(1), every.at[me, 1], {'tp': sib}
         elif k == 3:
             src, dst, dev = quarter(left, 0), quarter(left, 0), {'tp': right}
         elif k == 4:
@@ -232,9 +270,67 @@
             go(w, 7)
         go(w, 10)
 
-    def token_block(r):
-        to = lax.rem(me + r, tp)
-        return pltpu.make_async_remote_copy(src_ref=x_ref.at[to], dst_ref=xs_ref.at[me], send_sem=xsend.at[r], recv_sem=xrecv.at[r], device_id={'tp': to}, device_id_type=MESH)
+    def token_block(kind):
+        to, block, origin, relay = place.route(kind)
+        src = relay_ref.at[FORWARD.index(kind)] if kind in FORWARD else x_ref.at[block]
+        dst = xs_ref.at[origin] if relay is None else relay_ref.at[relay]
+        return pltpu.make_async_remote_copy(src_ref=src, dst_ref=dst, send_sem=xsend.at[kind], recv_sem=xrecv.at[SEAT[kind]], device_id={'tp': to}, device_id_type=MESH)
+
+    def tables(j):
+        quarter = cos4_ref.shape[1] // 4
+        lane4 = lax.broadcasted_iota(jnp.int32, cos4_ref.shape, 1)
+        rows_j = slice(j * cos4_ref.shape[0], (j + 1) * cos4_ref.shape[0])
+        sign = jnp.where(lane4 % head_dim < quarter, -1.0, 1.0).astype(F32)
+        for src, dst, factor in ((cos4_ref, cos_ref, None), (sin4_ref, sin_ref, sign)):
+            vals = jnp.where(lane4 // quarter == j, src[...], 0.0)
+            vals = vals + pltpu.roll(vals, quarter, 1)
+            vals = vals + pltpu.roll(vals, 2 * quarter, 1)
+            dst[rows_j, :] = vals if factor is None else vals * factor
+
+    def outputs(n):
+        block = lax.rem(n, 2)
+        at = pl.ds(pl.multiple_of(source(n) * tok, tok), tok)
+        return [
+            pltpu.make_async_copy(q_st.at[block], q_ref.at[:, at, :], out_sem.at[block, 0]),
+            pltpu.make_async_copy(k_st.at[block], k_ref.at[:, :, at], out_sem.at[block, 1]),
+            pltpu.make_async_copy(v_st.at[block], v_ref.at[:, at, :], out_sem.at[block, 2]),
+        ]
+
+    def source(n):
+        k = n // 2
+        hop = k + (k // 2) * (1 - 2 * (k % 2))
+        return lax.rem(me - core + 2 * hop, tp) + core + (n % 2) * (1 - 2 * core)
+
+    def project(direct, n, carry):
+        s, block = source(n), lax.rem(n, 2)
+        if not direct:
+            pltpu.make_async_remote_copy(src_ref=x_ref.at[0], dst_ref=xs_ref.at[s], send_sem=xsend.at[0], recv_sem=xrecv.at[n], device_id={'tp': right}, device_id_type=MESH).wait_recv()
+            for copy in outputs(n - 2):
+                copy.wait()
+        normed = norm_rows(xs_ref[s], again_ref[...], abias_ref[...])
+        at = pl.ds(pl.multiple_of(s * tok, tok), tok)
+        cos_tab, sin_tab = cos_ref[at, :], sin_ref[at, :]
+        lane = lax.broadcasted_iota(jnp.int32, (tok, pair), 1)
+        first = lane < head_dim
+        lane_mod = lane % head_dim
+
+        def rotate(vals):
+            vals = vals.astype(BF16).astype(F32)
+            return (vals * cos_tab + swap_halves(vals, lane_mod, head_dim // 2) * sin_tab).astype(BF16).astype(F32)
+
+        for p in range(tp // 2):
+            w = jnp.concatenate([wqkv_all[2 * p].reshape(width, 3 * pair), wqkv_all[2 * p + 1].reshape(width, 3 * pair)], axis=1)
+            both = jnp.dot(normed, w, preferred_element_type=F32)
+            for h in range(2):
+                t0, t1, t2 = [both[:, (3 * h + t) * pair:(3 * h + t + 1) * pair] for t in range(3)]
+                q_st[block, 2 * p + h] = (rotate(jnp.where(first, t0, t1)) * head_dim ** -0.5).astype(BF16)
+                keys = rotate(jnp.where(first, t2, t0)).T.astype(BF16)
+                k_st[block, 2 * p + h, :head_dim, :] = keys[head_dim:, :]
+                k_st[block, 2 * p + h, head_dim:, :] = keys[:head_dim, :]
+                v_st[block, 2 * p + h] = jnp.where(first, t1, t2).astype(BF16)
+        for copy in outputs(n):
+            copy.start()
+        return carry
 
     def gelu(pre):
         return (0.5 * pre * (1.0 + lax.erf(pre * (0.5 ** 0.5)))).astype(BF16)
@@ -269,63 +365,72 @@
     def halves(s, n):
         return up_all.at[s, n], down_all.at[s, n]
 
-    local = [
-        pltpu.make_async_copy(wqkv_ref, wqkv_all.at[me], own_sem.at[0]),
-        pltpu.make_async_copy(wo_ref, wo_all.at[me], own_sem.at[1]),
-        pltpu.make_async_copy(x_ref.at[me], xs_ref.at[me], own_sem.at[2]),
-    ]
+    local = pltpu.make_async_copy(wo_ref, wo_all.at[me], own_sem.at[0])
+    done = pltpu.make_async_copy(acc_ref, mlp_ref, own_sem.at[1])
     for w in (UP, DOWN, QKV, OUT):
         go(w, 0, 1, 2)
-    for copy in local:
-        copy.start()
+    go(UP, 14)
+    local.start()
+    token_block(2).start()
 
     def norm(t, carry):
-        tok = x_ref.shape[1]
-        m_ref[pl.ds(pl.multiple_of(t * tok, tok), tok), :] = norm_rows(x_ref[t], gain_ref[...], bias_ref[...])
+        m_ref[pl.ds(pl.multiple_of(t * tok, tok), tok), :] = norm_rows(x_ref[t], mgain_ref[...], mbias_ref[...])
         return carry
 
     lax.fori_loop(0, tp, norm, 0)
-    arrived(UP, 2)
+    arrived(UP, 2, 14)
     arrived(DOWN, 2)
     near(UP)
-    mlp(True, [(up_ref.at[0], down_ref.at[0]), (up_ref.at[1], down_ref.at[1]), halves(sib, 0), halves(sib, 1)])
+    mlp(True, [(up_cols(0), down_ref.at[0]), (up_cols(1), down_ref.at[1]), halves(sib, 0), halves(sib, 1)])
     near(DOWN)
-    distant(UP)
-    near(OUT)
     arrived(UP, 8, 9)
     arrived(DOWN, 8, 9)
-    sib_left, sib_right, sib_far = left + 1 - 2 * core, right + 1 - 2 * core, far + 1 - 2 * core
+    left_sib, right_sib, far_sib = place.left_sib, place.right_sib, place.far_sib
+    mlp(False, [halves(left, hz), halves(right, hz), halves(left_sib, hz), halves(right_sib, hz)])
+    near(OUT)
     near(QKV)
-    for r in range(1, tp):
-        token_block(r).start()
-    mlp(False, [halves(left, hz), halves(right, hz), halves(sib_left, hz), halves(sib_right, hz)])
+    for kind in (0, 1, 3, 4, 5, 6):
+        token_block(kind).start()
+    for j in range(4):
+        tables(j)
+    xs_ref[me] = x_ref[me]
+    wqkv_all[me] = wqkv_ref[...]
+    distant(UP)
     distant(DOWN)
-    distant(OUT)
-    distant(QKV)
     for w in (UP, DOWN):
         arrived(w, 5, 6)
         go(w, 11, 12)
     arrived(UP, 11, 12)
     arrived(DOWN, 11, 12)
-    mlp(False, [halves(left, 1 - hz), halves(right, 1 - hz), halves(sib_left, 1 - hz), halves(sib_right, 1 - hz)])
+    mlp(False, [halves(left, 1 - hz), halves(right, 1 - hz), halves(left_sib, 1 - hz), halves(right_sib, 1 - hz)])
+    distant(OUT)
+    distant(QKV)
+    for out, kind in zip(OUTWARD, FORWARD):
+        token_block(out).wait_recv()
+        token_block(kind).start()
     for w in (UP, DOWN):
         arrived(w, 7)
         go(w, 13)
+    arrived(QKV, 2, 8, 9, 10)
+    token_block(2).wait_recv()
+    lax.fori_loop(0, 2, functools.partial(project, True), 0)
     for w in (UP, DOWN):
         arrived(w, 10, 13)
-    mlp(False, [halves(far, hz), halves(far, 1 - hz), halves(sib_far, hz), halves(sib_far, 1 - hz)])
+    mlp(False, [halves(far, hz), halves(far, 1 - hz), halves(far_sib, hz), halves(far_sib, 1 - hz)])
+    done.start()
     arrived(OUT, 5, 6, 7)
     go(OUT, 11, 12, 13)
-    arrived(QKV, 2, 8, 9, 10)
+    lax.fori_loop(2, tp, functools.partial(project, False), 0)
+    for n in (6, 7):
+        for copy in outputs(n):
+            copy.wait()
     arrived(OUT, 2, 8, 9, 10, 11, 12, 13)
-    for r in range(1, tp):
-        token_block(r).wait_recv()
     for w, k in started:
         link(w, k).wait_send()
-    for r in range(1, tp):
-        token_block(r).wait_send()
-    for copy in local:
-        copy.wait()
+    for kind in range(9):
+        token_block(kind).wait_send()
+    local.wait()
+    done.wait()
 
 
 def final_kernel(x_ref, ctx_ref, wo_ref, mlp_ref, y_ref):
@@ -352,72 +457,51 @@
         tokens = batch * chunk
         half = head_dim // 2
 
-        w_qkv = w_qkv.reshape(width, groups, 3, head_dim).swapaxes(1, 2).reshape(width, 3 * pair)
+        inv_freq = 10000.0 ** (-2.0 * jnp.arange(half, dtype=F32) / head_dim)
+        reps = pair // half
+        pos4 = positions.astype(F32).reshape(reps, seq // reps)
+        angles = (pos4.T[:, :, None] * inv_freq[None, None, :]).reshape(seq // reps, pair)
         half_ff = ff // 2
         vmem = pl.BlockSpec(memory_space=pltpu.VMEM)
         hbm = pl.BlockSpec(memory_space=pl.ANY)
-        x_seq, wqkv_all, wo_all, mlp = pl.pallas_call(
-            functools.partial(exchange_kernel, 256),
-            in_specs=[vmem] * 7,
-            out_specs=[hbm, hbm, hbm, vmem],
+        q, k, v, wo_all, mlp = pl.pallas_call(
+            functools.partial(exchange_kernel, 256, head_dim),
+            in_specs=[vmem] * 11,
+            out_specs=[hbm] * 5,
             out_shape=[
-                jax.ShapeDtypeStruct((tp, chunk, width), BF16),
-                jax.ShapeDtypeStruct((tp, 2, width // 2, 3 * pair), BF16),
+                jax.ShapeDtypeStruct((tp, seq, pair), BF16),
+                jax.ShapeDtypeStruct((tp, pair, seq), BF16),
+                jax.ShapeDtypeStruct((tp, seq, pair), BF16),
                 jax.ShapeDtypeStruct((tp, 2, ctx_cols // 2, width), BF16),
                 jax.ShapeDtypeStruct((tokens, width), F32),
             ],
             scratch_shapes=[
+                pltpu.VMEM((tp, chunk, width), BF16),
+                pltpu.VMEM((tp, 2, width // 2, 3 * pair), BF16),
                 pltpu.VMEM((tp, 2, width, half_ff), BF16),
                 pltpu.VMEM((tp, 2, half_ff, width), BF16),
                 pltpu.VMEM((tokens, width), BF16),
-                pltpu.SemaphoreType.DMA((4, 14)),
-                pltpu.SemaphoreType.DMA((4, 14)),
-                pltpu.SemaphoreType.DMA((tp,)),
-                pltpu.SemaphoreType.DMA((tp,)),
-                pltpu.SemaphoreType.DMA((3,)),
+                pltpu.VMEM((tokens, width), F32),
+                pltpu.VMEM((2, chunk, width), BF16),
+                pltpu.VMEM((seq, pair), F32),
+                pltpu.VMEM((seq, pair), F32),
+                pltpu.VMEM((2, tp, chunk, pair), BF16),
+                pltpu.VMEM((2, tp, pair, chunk), BF16),
+                pltpu.VMEM((2, tp, chunk, pair), BF16),
+                pltpu.SemaphoreType.DMA((4, 15)),
+                pltpu.SemaphoreType.DMA((4, 15)),
+                pltpu.SemaphoreType.DMA((9,)),
+                pltpu.SemaphoreType.DMA((9,)),
+                pltpu.SemaphoreType.DMA((2,)),
+                pltpu.SemaphoreType.DMA((2, 3)),
             ],
             compiler_params=pltpu.CompilerParams(vmem_limit_bytes=VMEM_LIMIT, collective_id=0, has_side_effects=True),
             cost_estimate=pl.CostEstimate(flops=4 * tokens * width * ff * tp, bytes_accessed=4 * tokens * width * 2, transcendentals=0),
             name='exchange',
-        )(x, mlp_gain.reshape(1, width), mlp_bias.reshape(1, width),
-          w_up.reshape(width, 2, half_ff).swapaxes(0, 1), w_down.reshape(2, half_ff, width),
-          w_qkv.reshape(2, width // 2, 3 * pair), w_out.reshape(2, ctx_cols // 2, width))
-        wqkv_all = wqkv_all.reshape(tp, width, 3 * pair)
+        )(x, mlp_gain.reshape(1, width), mlp_bias.reshape(1, width), attn_gain.reshape(1, width), attn_bias.reshape(1, width),
+          w_up, w_down.reshape(2, half_ff, width),
+          w_qkv.reshape(2, width // 2, 3 * pair), w_out.reshape(2, ctx_cols // 2, width), jnp.cos(angles), jnp.sin(angles))
         wo_all = wo_all.reshape(tp * ctx_cols, width)
-
-        inv_freq = 10000.0 ** (-2.0 * jnp.arange(half, dtype=F32) / head_dim)
-        inv_freq = jnp.tile(inv_freq, 2 * groups)
-        angles = positions.astype(F32)[:, None] * inv_freq[None, :]
-        sign = jnp.where(jnp.arange(pair) % head_dim < half, -1.0, 1.0).astype(F32)
-        cos_tab, sin_tab = jnp.cos(angles), jnp.sin(angles) * sign[None, :]
-
-        gain2, bias2 = attn_gain.reshape(1, width), attn_bias.reshape(1, width)
-        nb = 2
-        q, k, v = pl.pallas_call(
-            functools.partial(qkv_kernel, head_dim),
-            grid=(tp // nb,),
-            in_specs=[
-                pl.BlockSpec((nb, chunk, width), lambda i: (i, 0, 0)),
-                pl.BlockSpec((tp, width, 3 * pair), lambda i: (0, 0, 0)),
-                pl.BlockSpec((nb * chunk, pair), lambda i: (i, 0)),
-                pl.BlockSpec((nb * chunk, pair), lambda i: (i, 0)),
-                pl.BlockSpec((1, width), lambda i: (0, 0)),
-                pl.BlockSpec((1, width), lambda i: (0, 0)),
-            ],
-            out_specs=[
-                pl.BlockSpec((tp, nb * chunk, pair), lambda i: (0, i, 0)),
-                pl.BlockSpec((tp, pair, nb * chunk), lambda i: (0, 0, i)),
-                pl.BlockSpec((tp, nb * chunk, pair), lambda i: (0, i, 0)),
-            ],
-            out_shape=[
-                jax.ShapeDtypeStruct((tp, seq, pair), BF16),
-                jax.ShapeDtypeStruct((tp, pair, seq), BF16),
-                jax.ShapeDtypeStruct((tp, seq, pair), BF16),
-            ],
-            compiler_params=params(('arbitrary',)),
-            cost_estimate=pl.CostEstimate(flops=2 * seq * width * 3 * pair * tp, bytes_accessed=2 * (seq * width * 4 + width * 3 * pair * tp), transcendentals=0),
-            name='qkv',
-        )(x_seq, wqkv_all, cos_tab, sin_tab, gain2, bias2)
 
         q_rows, kv_cols = 256, 512
         ctx = pl.pallas_call(
@@ -433,8 +517,9 @@
             scratch_shapes=[
                 pltpu.VMEM((2, q_rows, seq), F32),
                 pltpu.VMEM((2, seq, pair), BF16),
-                pltpu.SemaphoreType.DMA((2, tp)),
-                pltpu.SemaphoreType.DMA((tp, tp)),
+                pltpu.VMEM((tp, 2, chunk, pair), BF16),
+                pltpu.SemaphoreType.DMA((tp, 9)),
+                pltpu.SemaphoreType.DMA((tp, 9)),
                 pltpu.SemaphoreType.DMA((2,)),
             ],
             compiler_params=pltpu.CompilerParams(dimension_semantics=('arbitrary',), vmem_limit_bytes=VMEM_LIMIT, collective_id=1, has_side_effects=True),

time: 239 us -> 216 us (0.904)
  Pallas kernels: 227 us -> 209 us
  other arithmetic: 6.37 us -> 2.4 us
    pallas_call x2 -> x1, Pallas kernels: 145 us -> 126 us  [local_layer(): pl.pallas_call(functools.partial(exchange_kernel, 256, head_dim), in_spec...]
    mul x1 -> x0, other arithmetic: 5.59 us -> none  [local_layer(): cos_tab, sin_tab = (jnp.cos(angles), jnp.sin(angles) * sign[None, :])]
    another operation x3 -> x0, local copies, waits for them, and re-layouts: 2.44 us -> none  [the longest x2 2.44 us: local_layer(): w_qkv.reshape(2, width // 2, 3 * pair)]
where the time goes in v4:
time: 216 us
  Pallas kernels  209 us (97%)
  local copies, waits for them, and re-layouts  4.6 us (2%)
  other arithmetic  2.4 us (1%)
    pallas_call x1, Pallas kernels, local_layer(): pl.pallas_call(functools.partial(exchange_kernel, 256, head_dim), in_spec...  126 us
    pallas_call x1, Pallas kernels, local_layer(): pl.pallas_call(functools.partial(attn_kernel, head_dim, q_rows, kv_cols),...  70.9 us
    pallas_call x1, Pallas kernels, local_layer(): pl.pallas_call(final_kernel, grid=(nt,), in_specs=[pl.BlockSpec((rows, wi...  11.4 us
    reshape x2, local copies, waits for them, and re-layouts, local_layer(): w_qkv.reshape(2, width // 2, 3 * pair)  4.36 us

profile of v4, /device:TPU:81, one launch (start us, length us, event | category | flops | bytes accessed | tf_op | source)
XLA Modules:
  0.0 215.8 jit_solution(133568024033662852)
XLA Ops:
  0.0 0.1 mul.26
  0.1 0.7 convert_element_type.3
  0.8 0.1 copy.12
  1.0 1.7 multiply_sine_fusion
  2.7 2.6 %reshape.51 = bf16[2,512,384]{1,0,2:T(2,128)(2,1)S(1)} reshape(bf16[1024,2,192]{0,2,1:T(8,128)(2,1)} %param.15) | data formatting | bytes 1572864 | tf_op jit(solution)/shard_map/reshape | solution.py:503
  5.2 1.8 copy.13.wqkv_ref
  7.0 126.5 %exchange.1 = (bf16[8,2048,128]{2,1,0:T(8,128)(2,1)}, bf16[8,128,2048]{2,1,0:T(8,128)(2,1)}, bf16[8,2048,128]{2,1,0:T(8,128)(2,1)}, bf16[8,2,64,1024]{3,2,1,0:T(8,128)(2,1)}, f32[2048,1024]{1,0:T(8,128)}) custom-call(bf16[8,256,1024]{2,1,0:T(8,128)(2,1)} %x_ref.1, f32[1,1024]{1,0:T(1,128)} %bitcast.21, f32[1,1024]{1,0:T(1,128)} %bitcast.22, ...), custom_call_target="tpu_custom_call" | custom-call | flops 34359738368 | bytes 16777216 | tf_op jit(solution)/shard_map/exchange/pallas_call | solution.py:467
  133.5 70.9 %attn.1 = bf16[8,256,1024]{2,1,0:T(8,128)(2,1)} custom-call(bf16[8,2048,128]{2,1,0:T(8,128)(2,1)} %get-tuple-element.10.q_ref, bf16[8,128,2048]{2,1,0:T(8,128)(2,1)} %get-tuple-element.11.k_ref, bf16[8,2048,128]{2,1,0:T(8,128)(2,1)} %get-tuple-element.12.v_ref), custom_call_target="tpu_custom_call" | custom-call | flops 34359738368 | bytes 16777216 | tf_op jit(solution)/shard_map/attn/pallas_call | solution.py:507
  204.4 11.4 %final.1 = bf16[2048,1024]{1,0:T(8,128)(2,1)} custom-call(bf16[2048,1024]{1,0:T(8,128)(2,1)} %bitcast.14, bf16[2048,1024]{1,0:T(8,128)(2,1)} %bitcast.15, bf16[1024,1024]{1,0:T(8,128)(2,1)} %bitcast.16, f32[2048,1024]{1,0:T(8,128)} %get-tuple-element.14.mlp_ref), custom_call_target="tpu_custom_call" | custom-call | flops 4294967296 | bytes 20971520 | tf_op jit(solution)/shard_map/final/pallas_call | solution.py:533
  (4 shorter events, 0.0 us)

commit v5 on v4

--- a/solution.py
+++ b/solution.py
@@ -84,6 +84,11 @@
         for kind in DIRECT:
             ship(step, kind).wait_send()
         keep(step).wait()
+
+    def send_rows(start):
+        for kind in DIRECT:
+            mine = place.route(kind)[1] * tok // (seq // 2) == start // (seq // 2)
+            pl.when(mine)(ship(p, kind).start)
 
     def pass_on(step):
         for out, kind in zip(OUTWARD, FORWARD):
@@ -154,9 +159,10 @@
         r, h = unit
         out = (acc / jnp.sum(total, axis=1, keepdims=True)).astype(BF16)
         o_ref[slot, r:r + rows, h * head_dim:(h + 1) * head_dim] = out[:, h * head_dim:(h + 1) * head_dim]
-
-    for kind in DIRECT:
-        ship(p, kind).start()
+        if follow and r < seq // 2 <= follow[0]:
+            send_rows(0)
+
+    send_rows(seq // 2)
     keep(p).start()
 
     @pl.when(p >= 1)
@@ -319,8 +325,8 @@
             return (vals * cos_tab + swap_halves(vals, lane_mod, head_dim // 2) * sin_tab).astype(BF16).astype(F32)
 
         for p in range(tp // 2):
-            w = jnp.concatenate([wqkv_all[2 * p].reshape(width, 3 * pair), wqkv_all[2 * p + 1].reshape(width, 3 * pair)], axis=1)
-            both = jnp.dot(normed, w, preferred_element_type=F32)
+            w = wqkv_all[2 * p:2 * p + 2].reshape(6 * pair, width)
+            both = lax.dot_general(normed, w, (((1,), (1,)), ((), ())), preferred_element_type=F32)
             for h in range(2):
                 t0, t1, t2 = [both[:, (3 * h + t) * pair:(3 * h + t + 1) * pair] for t in range(3)]
                 q_st[block, 2 * p + h] = (rotate(jnp.where(first, t0, t1)) * head_dim ** -0.5).astype(BF16)
@@ -354,7 +360,7 @@
                 out = jnp.dot(act, down_w, preferred_element_type=F32)
                 rows_out = pl.ds(base + h * sub, sub)
                 if first:
-                    acc_ref[rows_out, :] = out
+                    acc_ref[rows_out, :] = out + x_ref[2 * t + h].astype(F32)
                 else:
                     acc_ref[rows_out, :] += out
                 pre = following
@@ -433,9 +439,9 @@
     done.wait()
 
 
-def final_kernel(x_ref, ctx_ref, wo_ref, mlp_ref, y_ref):
+def final_kernel(ctx_ref, wo_ref, rest_ref, y_ref):
     attn = jnp.dot(ctx_ref[...], wo_ref[...], preferred_element_type=F32)
-    y_ref[...] = (x_ref[...].astype(F32) + attn + mlp_ref[...]).astype(BF16)
+    y_ref[...] = (rest_ref[...] + attn).astype(BF16)
 
 
 def params(sem):
@@ -477,7 +483,7 @@
             ],
             scratch_shapes=[
                 pltpu.VMEM((tp, chunk, width), BF16),
-                pltpu.VMEM((tp, 2, width // 2, 3 * pair), BF16),
+                pltpu.VMEM((tp, groups, slot_cols, width), BF16),
                 pltpu.VMEM((tp, 2, width, half_ff), BF16),
                 pltpu.VMEM((tp, 2, half_ff, width), BF16),
                 pltpu.VMEM((tokens, width), BF16),
@@ -500,7 +506,7 @@
             name='exchange',
         )(x, mlp_gain.reshape(1, width), mlp_bias.reshape(1, width), attn_gain.reshape(1, width), attn_bias.reshape(1, width),
           w_up, w_down.reshape(2, half_ff, width),
-          w_qkv.reshape(2, width // 2, 3 * pair), w_out.reshape(2, ctx_cols // 2, width), jnp.cos(angles), jnp.sin(angles))
+          w_qkv.transpose(1, 2, 0), w_out.reshape(2, ctx_cols // 2, width), jnp.cos(angles), jnp.sin(angles))
         wo_all = wo_all.reshape(tp * ctx_cols, width)
 
         q_rows, kv_cols = 256, 512
@@ -527,14 +533,12 @@
             name='attn',
         )(q, k, v)
 
-        x_rows = x.reshape(tokens, width)
         rows = 512
         nt = tokens // rows
         y = pl.pallas_call(
             final_kernel,
             grid=(nt,),
             in_specs=[
-                pl.BlockSpec((rows, width), lambda t: (t, 0)),
                 pl.BlockSpec((rows, width), lambda t: (t, 0)),
                 pl.BlockSpec((width, width), lambda t: (0, 0)),
                 pl.BlockSpec((rows, width), lambda t: (t, 0)),
@@ -544,7 +548,7 @@
             compiler_params=params(('arbitrary',)),
             cost_estimate=pl.CostEstimate(flops=2 * tokens * width * width, bytes_accessed=tokens * width * 10, transcendentals=0),
             name='final',
-        )(x_rows, ctx.reshape(tokens, width), wo_all, mlp)
+        )(ctx.reshape(tokens, width), wo_all, mlp)
         return y.reshape(batch, chunk, width)
 
     return jax.shard_map(local_layer, mesh=mesh, in_specs=(P('dp', 'tp', None), P(), P(), P(), P(), P(None, 'tp', None), P('tp', None), P(None, 'tp'), P('tp', None), P()), out_specs=P('dp', 'tp', None), check_vma=False)

time: 216 us -> 212 us (0.981)
  local copies, waits for them, and re-layouts: 4.6 us -> 0.24 us
    reshape x2 -> x0, local copies, waits for them, and re-layouts: 4.36 us -> none  [local_layer(): w_qkv.reshape(2, width // 2, 3 * pair)]
where the time goes in v5:
time: 212 us
  Pallas kernels  209 us (99%)
  other arithmetic  2.38 us (1%)
    pallas_call x1, Pallas kernels, local_layer(): pl.pallas_call(functools.partial(exchange_kernel, 256, head_dim), in_spec...  127 us
    pallas_call x1, Pallas kernels, local_layer(): pl.pallas_call(functools.partial(attn_kernel, head_dim, q_rows, kv_cols),...  71.8 us
    pallas_call x1, Pallas kernels, local_layer(): pl.pallas_call(final_kernel, grid=(nt,), in_specs=[pl.BlockSpec((rows, wi...  10.2 us

profile of v5, /device:TPU:81, one launch (start us, length us, event | category | flops | bytes accessed | tf_op | source)
XLA Modules:
  0.0 211.9 jit_solution(12900994208369980740)
XLA Ops:
  0.0 0.1 mul.26
  0.1 0.7 convert_element_type.3
  0.8 0.1 copy.11
  1.0 1.7 multiply_sine_fusion
  2.6 127.2 %exchange.1 = (bf16[8,2048,128]{2,1,0:T(8,128)(2,1)}, bf16[8,128,2048]{2,1,0:T(8,128)(2,1)}, bf16[8,2048,128]{2,1,0:T(8,128)(2,1)}, bf16[8,2,64,1024]{3,2,1,0:T(8,128)(2,1)}, f32[2048,1024]{1,0:T(8,128)}) custom-call(bf16[8,256,1024]{2,1,0:T(8,128)(2,1)} %x_ref.1, f32[1,1024]{1,0:T(1,128)} %bitcast.19, f32[1,1024]{1,0:T(1,128)} %bitcast.20, ...), custom_call_target="tpu_custom_call" | custom-call | flops 34359738368 | bytes 16777216 | tf_op jit(solution)/shard_map/exchange/pallas_call | solution.py:473
  129.8 71.8 %attn.1 = bf16[8,256,1024]{2,1,0:T(8,128)(2,1)} custom-call(bf16[8,2048,128]{2,1,0:T(8,128)(2,1)} %get-tuple-element.10.q_ref, bf16[8,128,2048]{2,1,0:T(8,128)(2,1)} %get-tuple-element.11.k_ref, bf16[8,2048,128]{2,1,0:T(8,128)(2,1)} %get-tuple-element.12.v_ref), custom_call_target="tpu_custom_call" | custom-call | flops 34359738368 | bytes 16777216 | tf_op jit(solution)/shard_map/attn/pallas_call | solution.py:513
  201.7 10.2 %final.1 = bf16[2048,1024]{1,0:T(8,128)(2,1)} custom-call(bf16[2048,1024]{1,0:T(8,128)(2,1)} %bitcast.12, bf16[1024,1024]{1,0:T(8,128)(2,1)} %bitcast.13, f32[2048,1024]{1,0:T(8,128)} %get-tuple-element.14.rest_ref), custom_call_target="tpu_custom_call" | custom-call | flops 4294967296 | bytes 20971520 | tf_op jit(solution)/shard_map/final/pallas_call | solution.py:538
  (4 shorter events, 0.0 us)

commit v6 on v5

--- a/solution.py
+++ b/solution.py
@@ -14,7 +14,7 @@
 
 
 OUTWARD, FORWARD = (0, 1), (7, 8)
-SEAT = (0, 8, 1, 4, 2, 5, 3, 6, 7)
+SEAT = (0, 8, 1, 3, 2, 5, 4, 6, 7)
 DIRECT, LANDING = (0, 1, 2, 3, 4, 5, 6), (2, 3, 4, 5, 6, 7, 8)
 
 
@@ -67,18 +67,16 @@
 
     def ship(step, kind):
         to, block, origin, relay = place.route(kind)
-        lane_cols = pl.ds(pl.multiple_of(step * pair, pair), pair)
         if kind in FORWARD:
             src = relay_ref.at[step, FORWARD.index(kind)]
         else:
             src = o_ref.at[lax.rem(step, 2), pl.ds(pl.multiple_of(block * tok, tok), tok), :]
-        dst = ctx_ref.at[origin, :, lane_cols] if relay is None else relay_ref.at[step, relay]
+        dst = ctx_ref.at[origin, step] if relay is None else relay_ref.at[step, relay]
         return pltpu.make_async_remote_copy(src_ref=src, dst_ref=dst, send_sem=send.at[step, kind], recv_sem=recv.at[step, kind], device_id={'tp': to}, device_id_type=MESH)
 
     def keep(step):
-        lane_cols = pl.ds(pl.multiple_of(step * pair, pair), pair)
         src = o_ref.at[lax.rem(step, 2), pl.ds(pl.multiple_of(me * tok, tok), tok), :]
-        return pltpu.make_async_copy(src, ctx_ref.at[me, :, lane_cols], own_sem.at[lax.rem(step, 2)])
+        return pltpu.make_async_copy(src, ctx_ref.at[me, step], own_sem.at[lax.rem(step, 2)])
 
     def drain(step):
         for kind in DIRECT:
@@ -293,25 +291,30 @@
             vals = vals + pltpu.roll(vals, 2 * quarter, 1)
             dst[rows_j, :] = vals if factor is None else vals * factor
 
-    def outputs(n):
+    def outputs(n, s):
         block = lax.rem(n, 2)
-        at = pl.ds(pl.multiple_of(source(n) * tok, tok), tok)
+        at = pl.ds(pl.multiple_of(s * tok, tok), tok)
         return [
             pltpu.make_async_copy(q_st.at[block], q_ref.at[:, at, :], out_sem.at[block, 0]),
             pltpu.make_async_copy(k_st.at[block], k_ref.at[:, :, at], out_sem.at[block, 1]),
             pltpu.make_async_copy(v_st.at[block], v_ref.at[:, at, :], out_sem.at[block, 2]),
         ]
 
-    def source(n):
-        k = n // 2
-        hop = k + (k // 2) * (1 - 2 * (k % 2))
-        return lax.rem(me - core + 2 * hop, tp) + core + (n % 2) * (1 - 2 * core)
-
-    def project(direct, n, carry):
-        s, block = source(n), lax.rem(n, 2)
-        if not direct:
+    sources = (
+        lambda n: me + n * (1 - 2 * core),
+        lambda n: lax.rem(me + 2 + 4 * (n - 2), tp),
+        lambda n: place.other(lax.rem(me + 2 + 4 * (n - 4), tp)),
+        lambda n: far + (n - 6) * (1 - 2 * core),
+    )
+
+    def project_pair(g):
+        lax.fori_loop(2 * g, 2 * g + 2, functools.partial(project, g), 0)
+
+    def project(g, n, carry):
+        s, block = sources[g](n), lax.rem(n, 2)
+        if g > 0:
             pltpu.make_async_remote_copy(src_ref=x_ref.at[0], dst_ref=xs_ref.at[s], send_sem=xsend.at[0], recv_sem=xrecv.at[n], device_id={'tp': right}, device_id_type=MESH).wait_recv()
-            for copy in outputs(n - 2):
+            for copy in outputs(n - 2, sources[g - 1](n - 2)):
                 copy.wait()
         normed = norm_rows(xs_ref[s], again_ref[...], abias_ref[...])
         at = pl.ds(pl.multiple_of(s * tok, tok), tok)
@@ -334,7 +337,7 @@
                 k_st[block, 2 * p + h, :head_dim, :] = keys[head_dim:, :]
                 k_st[block, 2 * p + h, head_dim:, :] = keys[:head_dim, :]
                 v_st[block, 2 * p + h] = jnp.where(first, t1, t2).astype(BF16)
-        for copy in outputs(n):
+        for copy in outputs(n, s):
             copy.start()
         return carry
 
@@ -393,7 +396,6 @@
     arrived(DOWN, 8, 9)
     left_sib, right_sib, far_sib = place.left_sib, place.right_sib, place.far_sib
     mlp(False, [halves(left, hz), halves(right, hz), halves(left_sib, hz), halves(right_sib, hz)])
-    near(OUT)
     near(QKV)
     for kind in (0, 1, 3, 4, 5, 6):
         token_block(kind).start()
@@ -409,26 +411,29 @@
     arrived(UP, 11, 12)
     arrived(DOWN, 11, 12)
     mlp(False, [halves(left, 1 - hz), halves(right, 1 - hz), halves(left_sib, 1 - hz), halves(right_sib, 1 - hz)])
-    distant(OUT)
+    near(OUT)
     distant(QKV)
     for out, kind in zip(OUTWARD, FORWARD):
         token_block(out).wait_recv()
         token_block(kind).start()
+    arrived(QKV, 2, 8, 9, 10)
+    token_block(2).wait_recv()
+    project_pair(0)
+    distant(OUT)
+    project_pair(1)
     for w in (UP, DOWN):
         arrived(w, 7)
         go(w, 13)
-    arrived(QKV, 2, 8, 9, 10)
-    token_block(2).wait_recv()
-    lax.fori_loop(0, 2, functools.partial(project, True), 0)
     for w in (UP, DOWN):
         arrived(w, 10, 13)
     mlp(False, [halves(far, hz), halves(far, 1 - hz), halves(far_sib, hz), halves(far_sib, 1 - hz)])
     done.start()
     arrived(OUT, 5, 6, 7)
     go(OUT, 11, 12, 13)
-    lax.fori_loop(2, tp, functools.partial(project, False), 0)
+    project_pair(2)
+    project_pair(3)
     for n in (6, 7):
-        for copy in outputs(n):
+        for copy in outputs(n, sources[3](n)):
             copy.wait()
     arrived(OUT, 2, 8, 9, 10, 11, 12, 13)
     for w, k in started:
@@ -440,7 +445,9 @@
 
 
 def final_kernel(ctx_ref, wo_ref, rest_ref, y_ref):
-    attn = jnp.dot(ctx_ref[...], wo_ref[...], preferred_element_type=F32)
+    ctx = jnp.concatenate([
+        jnp.concatenate([ctx_ref[b, p] for p in range(ctx_ref.shape[1])], axis=1) for b in range(ctx_ref.shape[0])], axis=0)
+    attn = jnp.dot(ctx, wo_ref[...], preferred_element_type=F32)
     y_ref[...] = (rest_ref[...] + attn).astype(BF16)
 
 
@@ -519,7 +526,7 @@
                 pl.BlockSpec((1, seq, pair), lambda p: (p, 0, 0)),
             ],
             out_specs=hbm,
-            out_shape=jax.ShapeDtypeStruct((tp, chunk, tp * pair), BF16),
+            out_shape=jax.ShapeDtypeStruct((tp, tp, chunk, pair), BF16),
             scratch_shapes=[
                 pltpu.VMEM((2, q_rows, seq), F32),
                 pltpu.VMEM((2, seq, pair), BF16),
@@ -539,7 +546,7 @@
             final_kernel,
             grid=(nt,),
             in_specs=[
-                pl.BlockSpec((rows, width), lambda t: (t, 0)),
+                pl.BlockSpec((rows // chunk, tp, chunk, pair), lambda t: (t, 0, 0, 0)),
                 pl.BlockSpec((width, width), lambda t: (0, 0)),
                 pl.BlockSpec((rows, width), lambda t: (t, 0)),
             ],
@@ -548,7 +555,7 @@
             compiler_params=params(('arbitrary',)),
             cost_estimate=pl.CostEstimate(flops=2 * tokens * width * width, bytes_accessed=tokens * width * 10, transcendentals=0),
             name='final',
-        )(ctx.reshape(tokens, width), wo_all, mlp)
+        )(ctx, wo_all, mlp)
         return y.reshape(batch, chunk, width)
 
     return jax.shard_map(local_layer, mesh=mesh, in_specs=(P('dp', 'tp', None), P(), P(), P(), P(), P(None, 'tp', None), P('tp', None), P(None, 'tp'), P('tp', None), P()), out_specs=P('dp', 'tp', None), check_vma=False)

time: 212 us -> 218 us (1.028)
  Pallas kernels: 209 us -> 216 us
    pallas_call x1, Pallas kernels: 127 us -> 138 us  [local_layer(): pl.pallas_call(functools.partial(exchange_kernel, 256, head_dim), in_spec...]
    pallas_call x1, Pallas kernels: 71.8 us -> 67.8 us  [local_layer(): pl.pallas_call(functools.partial(attn_kernel, head_dim, q_rows, kv_cols),...]
where the time goes in v6:
time: 218 us
  Pallas kernels  216 us (99%)
  other arithmetic  2.38 us (1%)
    pallas_call x1, Pallas kernels, local_layer(): pl.pallas_call(functools.partial(exchange_kernel, 256, head_dim), in_spec...  138 us
    pallas_call x1, Pallas kernels, local_layer(): pl.pallas_call(functools.partial(attn_kernel, head_dim, q_rows, kv_cols),...  67.8 us
    pallas_call x1, Pallas kernels, local_layer(): pl.pallas_call(final_kernel, grid=(nt,), in_specs=[pl.BlockSpec((rows //...  9.89 us

profile of v6, /device:TPU:81, one launch (start us, length us, event | category | flops | bytes accessed | tf_op | source)
XLA Modules:
  0.0 218.3 jit_solution(4351845024093190892)
XLA Ops:
  0.0 0.1 mul.26
  0.1 0.7 convert_element_type.3
  0.8 0.1 copy.11
  1.0 1.7 multiply_sine_fusion
  2.6 138.0 %exchange.1 = (bf16[8,2048,128]{2,1,0:T(8,128)(2,1)}, bf16[8,128,2048]{2,1,0:T(8,128)(2,1)}, bf16[8,2048,128]{2,1,0:T(8,128)(2,1)}, bf16[8,2,64,1024]{3,2,1,0:T(8,128)(2,1)}, f32[2048,1024]{1,0:T(8,128)}) custom-call(bf16[8,256,1024]{2,1,0:T(8,128)(2,1)} %x_ref.1, f32[1,1024]{1,0:T(1,128)} %bitcast.17, f32[1,1024]{1,0:T(1,128)} %bitcast.18, ...), custom_call_target="tpu_custom_call" | custom-call | flops 34359738368 | bytes 16777216 | tf_op jit(solution)/shard_map/exchange/pallas_call | solution.py:480
  140.6 67.8 %attn.1.ctx_ref = bf16[8,8,256,128]{3,2,1,0:T(8,128)(2,1)} custom-call(bf16[8,2048,128]{2,1,0:T(8,128)(2,1)} %get-tuple-element.10.q_ref, bf16[8,128,2048]{2,1,0:T(8,128)(2,1)} %get-tuple-element.11.k_ref, bf16[8,2048,128]{2,1,0:T(8,128)(2,1)} %get-tuple-element.12.v_ref), custom_call_target="tpu_custom_call" | custom-call | flops 34359738368 | bytes 16777216 | tf_op jit(solution)/shard_map/attn/pallas_call | solution.py:520
  208.4 9.9 %final.1 = bf16[2048,1024]{1,0:T(8,128)(2,1)} custom-call(bf16[8,8,256,128]{3,2,1,0:T(8,128)(2,1)} %attn.1.ctx_ref, bf16[1024,1024]{1,0:T(8,128)(2,1)} %bitcast.11, f32[2048,1024]{1,0:T(8,128)} %get-tuple-element.14.rest_ref), custom_call_target="tpu_custom_call" | custom-call | flops 4294967296 | bytes 20971520 | tf_op jit(solution)/shard_map/final/pallas_call | solution.py:545
  (4 shorter events, 0.0 us)

commit v7 on v6

--- a/solution.py
+++ b/solution.py
@@ -420,7 +420,6 @@
     token_block(2).wait_recv()
     project_pair(0)
     distant(OUT)
-    project_pair(1)
     for w in (UP, DOWN):
         arrived(w, 7)
         go(w, 13)
@@ -430,6 +429,7 @@
     done.start()
     arrived(OUT, 5, 6, 7)
     go(OUT, 11, 12, 13)
+    project_pair(1)
     project_pair(2)
     project_pair(3)
     for n in (6, 7):

time: 218 us -> 219 us (level)
  no operation moved by 1% of the time
where the time goes in v7:
time: 219 us; the launch traced here: 218 us
  Pallas kernels  216 us (99%)
  other arithmetic  2.38 us (1%)
    pallas_call x1, Pallas kernels, local_layer(): pl.pallas_call(functools.partial(exchange_kernel, 256, head_dim), in_spec...  138 us
    pallas_call x1, Pallas kernels, local_layer(): pl.pallas_call(functools.partial(attn_kernel, head_dim, q_rows, kv_cols),...  67.8 us
    pallas_call x1, Pallas kernels, local_layer(): pl.pallas_call(final_kernel, grid=(nt,), in_specs=[pl.BlockSpec((rows //...  9.89 us

profile of v7, /device:TPU:81, one launch (start us, length us, event | category | flops | bytes accessed | tf_op | source)
XLA Modules:
  0.0 218.5 jit_solution(221734268010770267)
XLA Ops:
  0.0 0.1 mul.26
  0.1 0.7 convert_element_type.3
  0.8 0.1 copy.11
  1.0 1.7 multiply_sine_fusion
  2.6 138.2 %exchange.1 = (bf16[8,2048,128]{2,1,0:T(8,128)(2,1)}, bf16[8,128,2048]{2,1,0:T(8,128)(2,1)}, bf16[8,2048,128]{2,1,0:T(8,128)(2,1)}, bf16[8,2,64,1024]{3,2,1,0:T(8,128)(2,1)}, f32[2048,1024]{1,0:T(8,128)}) custom-call(bf16[8,256,1024]{2,1,0:T(8,128)(2,1)} %x_ref.1, f32[1,1024]{1,0:T(1,128)} %bitcast.17, f32[1,1024]{1,0:T(1,128)} %bitcast.18, ...), custom_call_target="tpu_custom_call" | custom-call | flops 34359738368 | bytes 16777216 | tf_op jit(solution)/shard_map/exchange/pallas_call | solution.py:480
  140.8 67.8 %attn.1.ctx_ref = bf16[8,8,256,128]{3,2,1,0:T(8,128)(2,1)} custom-call(bf16[8,2048,128]{2,1,0:T(8,128)(2,1)} %get-tuple-element.10.q_ref, bf16[8,128,2048]{2,1,0:T(8,128)(2,1)} %get-tuple-element.11.k_ref, bf16[8,2048,128]{2,1,0:T(8,128)(2,1)} %get-tuple-element.12.v_ref), custom_call_target="tpu_custom_call" | custom-call | flops 34359738368 | bytes 16777216 | tf_op jit(solution)/shard_map/attn/pallas_call | solution.py:520
  208.6 9.9 %final.1 = bf16[2048,1024]{1,0:T(8,128)(2,1)} custom-call(bf16[8,8,256,128]{3,2,1,0:T(8,128)(2,1)} %attn.1.ctx_ref, bf16[1024,1024]{1,0:T(8,128)(2,1)} %bitcast.11, f32[2048,1024]{1,0:T(8,128)} %get-tuple-element.14.rest_ref), custom_call_target="tpu_custom_call" | custom-call | flops 4294967296 | bytes 20971520 | tf_op jit(solution)/shard_map/final/pallas_call | solution.py:545
  (4 shorter events, 0.0 us)
